TPU v7x, 32 devices: a whole 2x2x4 slice. The times are simulated.
32 devices in a mesh: z: 4 (over z), y: 2 (over y), x: 4 (over x, core).
Axes of the slice: x: 2, y: 2, z: 4, core: 2. Of those that a mesh axis runs over, the one named last changes fastest.
Arguments:
- atom_pos: float32 [23328, 3], P(('z', 'y', 'x'))
- atom_vel: float32 [23328, 3], P(('z', 'y', 'x'))
- atom_frc: float32 [23328, 3], P(('z', 'y', 'x'))
- atom_id: int32 [23328], P(('z', 'y', 'x'))
- atom_ok: int32 [23328], P(('z', 'y', 'x'))
- brick_side: float32 [], replicated
Outputs:
- output 1: float32 [23328, 3], P(('z', 'y', 'x'))
- output 2: float32 [23328, 3], P(('z', 'y', 'x'))
- output 3: float32 [23328, 3], P(('z', 'y', 'x'))
- output 4: int32 [23328], P(('z', 'y', 'x'))
- output 5: int32 [23328], P(('z', 'y', 'x'))
- output 6: float32 [], replicated
All inputs are finite; a program needn't handle non-finite values.
Results may differ from a plain program's by a relative error of at most 0.001.
Values sent between devices are 32-bit elements.
A program may use at most 1 GiB of HBM per device.

v0:
```python
import jax
import jax.numpy as jnp
from jax import lax
from jax.sharding import PartitionSpec as P

DT = 0.005
RC = 2.5
FAR_AWAY = 1.0e6
UCUT = 4.0 * (RC ** -12 - RC ** -6)
UPC = -48.0 * RC ** -13 + 24.0 * RC ** -7
MESH_AXES = ("z", "y", "x")
ALL_DIRS = [(step_x, step_y, step_z) for step_z in (-1, 0, 1) for step_y in (-1, 0, 1) for step_x in (-1, 0, 1) if (step_x, step_y, step_z) != (0, 0, 0)]
UPPER_DIRS = [direction for direction in ALL_DIRS if direction[2] > 0 or (direction[2] == 0 and (direction[1] > 0 or (direction[1] == 0 and direction[0] > 0)))]


def shift_perm(mesh_sizes, direction):
    size_z, size_y, size_x = mesh_sizes
    return [((pos_z * size_y + pos_y) * size_x + pos_x, (((pos_z + direction[2]) % size_z) * size_y + (pos_y + direction[1]) % size_y) * size_x + (pos_x + direction[0]) % size_x) for pos_z in range(size_z) for pos_y in range(size_y) for pos_x in range(size_x)]


def dir_code(direction):
    return (direction[2] + 1) * 9 + (direction[1] + 1) * 3 + (direction[0] + 1)


def pair_block(own_pos, other_pos, pair_ok):
    delta_r = own_pos[:, None, :] - other_pos[None, :, :]
    dist_sq = jnp.sum(delta_r * delta_r, axis=-1)
    in_range = pair_ok & (dist_sq < RC * RC)
    safe_sq = jnp.where(in_range, dist_sq, 1.0)
    inv_r2 = 1.0 / safe_sq
    inv_r6 = inv_r2 * inv_r2 * inv_r2
    radius = jnp.sqrt(safe_sq)
    f_scale = jnp.where(in_range, (48.0 * inv_r6 * inv_r6 - 24.0 * inv_r6) * inv_r2 + UPC / radius, 0.0)
    pair_energy = jnp.where(in_range, 4.0 * (inv_r6 * inv_r6 - inv_r6) - UCUT - (radius - RC) * UPC, 0.0)
    return f_scale[:, :, None] * delta_r, jnp.sum(pair_energy)


def solution(mesh):
    size_z = mesh.shape["z"]
    size_y = mesh.shape["y"]
    size_x = mesh.shape["x"]
    mesh_sizes = (size_z, size_y, size_x)

    def local_step(atom_pos, atom_vel, atom_frc, atom_id, atom_ok, brick_side):
        capacity = atom_pos.shape[0]
        move_cap = max(1, capacity // 100)
        my_brick = jnp.stack([lax.axis_index("x"), lax.axis_index("y"), lax.axis_index("z")]).astype(jnp.int32)
        dims_int = jnp.array([size_x, size_y, size_z], jnp.int32)
        box_len = brick_side * dims_int.astype(jnp.float32)
        owned = atom_ok > 0
        half_v = atom_vel + (0.5 * DT) * atom_frc
        unwrapped = atom_pos + DT * half_v
        moved = jnp.mod(unwrapped, box_len)
        step_vec = jnp.clip(jnp.floor(unwrapped / brick_side).astype(jnp.int32) - my_brick, -1, 1)
        code_all = (step_vec[:, 2] + 1) * 9 + (step_vec[:, 1] + 1) * 3 + (step_vec[:, 0] + 1)
        code_all = jnp.where(owned, code_all, -1)
        dir_codes = jnp.array([dir_code(direction) for direction in ALL_DIRS], jnp.int32)
        member = code_all[None, :] == dir_codes[:, None]
        member_rank = jnp.cumsum(member.astype(jnp.int32), axis=1) - 1
        pick_mask = member[:, None, :] & (member_rank[:, None, :] == jnp.arange(move_cap)[None, :, None])
        source_row = jnp.sum(jnp.where(pick_mask, jnp.arange(capacity)[None, None, :], 0), axis=-1)
        filled = jnp.any(pick_mask, axis=-1)
        packet = jnp.concatenate([moved[source_row], half_v[source_row], filled[..., None].astype(jnp.float32)], axis=-1)
        packet = jnp.where(filled[..., None], packet, 0.0)
        packet_id = jnp.where(filled, atom_id[source_row], 0)
        arrived = []
        arrived_id = []
        for dir_index, direction in enumerate(ALL_DIRS):
            perm_pairs = shift_perm(mesh_sizes, direction)
            arrived.append(lax.ppermute(packet[dir_index], MESH_AXES, perm_pairs))
            arrived_id.append(lax.ppermute(packet_id[dir_index], MESH_AXES, perm_pairs))
        arrived = jnp.concatenate(arrived, axis=0)
        arrived_id = jnp.concatenate(arrived_id, axis=0)
        staying = code_all == dir_code((0, 0, 0))
        cand_pos = jnp.concatenate([moved, arrived[:, 0:3]], axis=0)
        cand_vel = jnp.concatenate([half_v, arrived[:, 3:6]], axis=0)
        cand_id = jnp.concatenate([atom_id, arrived_id], axis=0)
        cand_ok = jnp.concatenate([staying, arrived[:, 6] > 0.5], axis=0)
        keep_order = jnp.argsort(jnp.where(cand_ok, cand_id, 2147483647))[:capacity]
        new_ok = cand_ok[keep_order]
        ok_f = new_ok[:, None].astype(jnp.float32)
        new_pos = cand_pos[keep_order] * ok_f
        new_half = cand_vel[keep_order] * ok_f
        new_id = jnp.where(new_ok, cand_id[keep_order], 0)
        local_pos = new_pos - my_brick.astype(jnp.float32) * brick_side
        ghost_in = []
        for direction in UPPER_DIRS:
            near_face = new_ok
            image_shift = []
            for axis_d in range(3):
                if direction[axis_d] == 1:
                    near_face = near_face & (local_pos[:, axis_d] < RC)
                    image_shift.append(jnp.where(my_brick[axis_d] == 0, box_len[axis_d], 0.0))
                elif direction[axis_d] == -1:
                    near_face = near_face & (local_pos[:, axis_d] > brick_side - RC)
                    image_shift.append(jnp.where(my_brick[axis_d] == dims_int[axis_d] - 1, -box_len[axis_d], 0.0))
                else:
                    image_shift.append(jnp.zeros((), jnp.float32))
            ghost_out = jnp.where(near_face[:, None], new_pos + jnp.stack(image_shift), FAR_AWAY)
            back_dir = tuple(-component for component in direction)
            ghost_in.append(lax.ppermute(ghost_out, MESH_AXES, shift_perm(mesh_sizes, back_dir)))
        slot_ids = jnp.arange(capacity)
        self_ok = new_ok[:, None] & new_ok[None, :] & (slot_ids[:, None] != slot_ids[None, :])
        pair_force, pair_energy = pair_block(new_pos, new_pos, self_ok)
        force_sum = jnp.sum(pair_force, axis=1)
        energy_sum = 0.5 * pair_energy
        reactions = []
        for dir_index in range(len(UPPER_DIRS)):
            pair_force, pair_energy = pair_block(new_pos, ghost_in[dir_index], new_ok[:, None])
            force_sum = force_sum + jnp.sum(pair_force, axis=1)
            energy_sum = energy_sum + pair_energy
            reactions.append(-jnp.sum(pair_force, axis=0))
        for dir_index, direction in enumerate(UPPER_DIRS):
            force_sum = force_sum + lax.ppermute(reactions[dir_index], MESH_AXES, shift_perm(mesh_sizes, direction))
        energy = lax.psum(energy_sum, MESH_AXES)
        new_force = force_sum * ok_f
        new_vel = (new_half + (0.5 * DT) * new_force) * ok_f
        return new_pos, new_vel, new_force, new_id, new_ok.astype(jnp.int32), energy

    row_spec = P(MESH_AXES, None)
    id_spec = P(MESH_AXES)
    return jax.shard_map(local_step, mesh=mesh, in_specs=(row_spec, row_spec, row_spec, id_spec, id_spec, P()), out_specs=(row_spec, row_spec, row_spec, id_spec, id_spec, P()), check_vma=False)
```

profile of v0, /device:TPU:0, one launch (start us, length us, event | category | flops | bytes accessed | tf_op | source)
XLA Modules:
  0.0 303.2 jit_solution(18398016713995956099)
XLA Ops:
  10.6 6.5 %collective-permute-start.32 = (s32[7]{0:T(128)S(1)}, s32[7]{0:T(128)S(1)}, u32[]{:S(2)}, u32[]{:S(2)}) collective-permute-start(s32[7]{0:T(128)S(1)} %get-tuple-element.199), channel_id=1, source_target_pairs={{0,31},{1,28},{2,29},{3,30},{4,27},{5,24},{6,25},{7,26},{8,7},{9,4... | collective-permute-start | bytes 92 | tf_op jit(solution)/shard_map/ppermute | solution.py:71
  41.4 3.4 %collective-permute-start.46 = (s32[7]{0:T(128)S(1)}, s32[7]{0:T(128)S(1)}, u32[]{:S(2)}, u32[]{:S(2)}) collective-permute-start(s32[7]{0:T(128)S(1)} %get-tuple-element.185), channel_id=1, source_target_pairs={{0,11},{1,8},{2,9},{3,10},{4,15},{5,12},{6,13},{7,14},{8,19},{9,16... | collective-permute-start | bytes 92 | tf_op jit(solution)/shard_map/ppermute | solution.py:71
  45.2 4.2 %collective-permute-start.43 = (s32[7]{0:T(128)S(1)}, s32[7]{0:T(128)S(1)}, u32[]{:S(2)}, u32[]{:S(2)}) collective-permute-start(s32[7]{0:T(128)S(1)} %get-tuple-element.188), channel_id=1, source_target_pairs={{0,15},{1,12},{2,13},{3,14},{4,11},{5,8},{6,9},{7,10},{8,23},{9,20... | collective-permute-start | bytes 92 | tf_op jit(solution)/shard_map/ppermute | solution.py:71
  69.1 2.7 collective-permute-start.14
  72.6 3.0 collective-permute-start.17
  77.7 3.7 %collective-permute-start.20 = (f32[7,7]{1,0:T(8,128)S(1)}, f32[7,7]{1,0:T(8,128)S(1)}, u32[]{:S(2)}, u32[]{:S(2)}) collective-permute-start(f32[7,7]{1,0:T(8,128)S(1)} %bitcast.118), channel_id=1, source_target_pairs={{0,11},{1,8},{2,9},{3,10},{4,15},{5,12},{6,13},{7,14},{8,19},{9,16... | collective-permute-start | bytes 596 | tf_op jit(solution)/shard_map/ppermute | solution.py:70
  82.6 3.4 %collective-permute-start.23 = (f32[7,7]{1,0:T(8,128)S(1)}, f32[7,7]{1,0:T(8,128)S(1)}, u32[]{:S(2)}, u32[]{:S(2)}) collective-permute-start(f32[7,7]{1,0:T(8,128)S(1)} %bitcast.115), channel_id=1, source_target_pairs={{0,15},{1,12},{2,13},{3,14},{4,11},{5,8},{6,9},{7,10},{8,23},{9,20... | collective-permute-start | bytes 596 | tf_op jit(solution)/shard_map/ppermute | solution.py:70
  91.0 2.6 collective-permute-start.2
  98.6 4.2 %collective-permute-start.6 = (f32[7,7]{1,0:T(8,128)S(1)}, f32[7,7]{1,0:T(8,128)S(1)}, u32[]{:S(2)}, u32[]{:S(2)}) collective-permute-start(f32[7,7]{1,0:T(8,128)S(1)} %bitcast.106), channel_id=1, source_target_pairs={{0,31},{1,28},{2,29},{3,30},{4,27},{5,24},{6,25},{7,26},{8,7},{9,4... | collective-permute-start | bytes 596 | tf_op jit(solution)/shard_map/ppermute | solution.py:70
  104.4 4.4 %sort.17 = (s32[911]{0:T(1024)}, s32[911]{0:T(1024)S(1)}) sort(s32[911]{0:T(1024)S(1)} %get-tuple-element.136, s32[911]{0:T(1024)S(1)} %iota.28), dimensions={0}, to_apply=%region_4.5 | sort | flops 9110 | bytes 14576 | tf_op jit(solution)/shard_map/jit(argsort)/sort | solution.py:79
  108.8 3.2 %gather_fusion.6 = s32[729]{0:T(1024)S(1)} fusion(s32[911]{0:T(1024)S(1)} %concatenate.26, s32[1024]{0:T(1024)S(1)} %pad_clamp_fusion), kind=kCustom, calls=%fused_computation.6 | custom fusion | bytes 8748 | tf_op jit(solution)/shard_map/gather | solution.py:84
  112.0 5.0 %gather_fusion.4 = pred[729]{0:T(1024)(128)(4,1)S(1)} fusion(pred[911]{0:T(1024)(128)(4,1)S(1)} %get-tuple-element.137, s32[1024]{0:T(1024)S(1)} %pad_clamp_fusion), kind=kCustom, calls=%fused_computation.4 | custom fusion | bytes 4374 | tf_op jit(solution)/shard_map/gather | solution.py:80
  124.6 4.2 %collective-permute-start.64 = (f32[729,3]{0,1:T(4,128)S(1)}, f32[729,3]{0,1:T(4,128)S(1)}, u32[]{:S(2)}, u32[]{:S(2)}) collective-permute-start(f32[729,3]{0,1:T(4,128)S(1)} %get-tuple-element.207), channel_id=1, source_target_pairs={{0,31},{1,28},{2,29},{3,30},{4,27},{5,24},{6,25},{7,26},{8,7},{9,4... | collective-permute-start | bytes 26252 | tf_op jit(solution)/shard_map/ppermute | solution.py:101
  133.8 3.5 %collective-permute-start.60 = (f32[729,3]{0,1:T(4,128)S(1)}, f32[729,3]{0,1:T(4,128)S(1)}, u32[]{:S(2)}, u32[]{:S(2)}) collective-permute-start(f32[729,3]{0,1:T(4,128)S(1)} %get-tuple-element.211), channel_id=1, source_target_pairs={{0,24},{1,25},{2,26},{3,27},{4,28},{5,29},{6,30},{7,31},{8,0},{9,1... | collective-permute-start | bytes 26252 | tf_op jit(solution)/shard_map/ppermute | solution.py:101
  142.4 4.6 %fusion.44 = (f32[729,729]{1,0:T(8,128)}, f32[729,729]{1,0:T(8,128)}) fusion(f32[729,729]{1,0:T(8,128)S(1)} %get-tuple-element.89, pred[729]{0:T(1024)(128)(4,1)S(1)} %gather_fusion.4, f32[729,729]{1,0:T(8,128)S(1)} %get-tuple-element.90), kind=kLoop, calls=%fused_computation.121 | loop fusion | flops 16474671 | bytes 8503785 | tf_op jit(solution)/shard_map/jit(_where)/select_n | solution.py:33
  147.0 25.6 %fusion.1 = (f32[729,3]{0,1:T(4,128)S(1)}, f32[729,3]{0,1:T(4,128)S(1)}, f32[729,729]{1,0:T(8,128)S(1)}, f32[729,729]{1,0:T(8,128)S(1)}, f32[729,729]{1,0:T(8,12...) fusion(f32[729,729]{1,0:T(8,128)} %get-tuple-element.225, ...), kind=kLoop, calls=%fused_computation.36 | loop fusion | flops 62172040 | bytes 29909412 | tf_op jit(solution)/shard_map/reduce_sum | solution.py:110
  175.1 42.5 %fusion.166 = (f32[]{:T(128)}, f32[]{:T(128)}, f32[]{:T(128)}, f32[]{:T(128)}, f32[]{:T(128)}, /*index=5*/f32[]{:T(128)}, f32[]{:T(128)}, f32[]{:T(128)}, f32[]{...) fusion(f32[729,729]{1,0:T(8,128)} %get-tuple-element.87, ...), kind=kLoop, calls=%fused_computation.243 | loop fusion | flops 164214992 | bytes 55270648 | tf_op jit(solution)/shard_map/reduce_sum | solution.py:35
  217.6 11.5 %fusion.3 = (f32[729,3]{0,1:T(4,128)S(1)}, f32[729,3]{0,1:T(4,128)S(1)}, f32[729,3]{0,1:T(4,128)S(1)}, f32[729,3]{0,1:T(4,128)S(1)}, f32[729,3]{0,1:T(4,128)S(1)...) fusion(f32[729,729]{1,0:T(8,128)S(1)} %get-tuple-element.152, ...), kind=kLoop, calls=%fused_computation.38 | loop fusion | flops 57356272 | bytes 19376820 | tf_op jit(solution)/shard_map/reduce_sum | solution.py:110
  229.9 3.6 %collective-permute-start.72 = (f32[729,3]{0,1:T(4,128)S(1)}, f32[729,3]{0,1:T(4,128)S(1)}, u32[]{:S(2)}, u32[]{:S(2)}) collective-permute-start(f32[729,3]{0,1:T(4,128)S(1)} %neg.59), channel_id=1, source_target_pairs={{0,11},{1,8},{2,9},{3,10},{4,15},{5,12},{6,13},{7,14},{8,19},{9,16... | collective-permute-start | bytes 26252 | tf_op jit(solution)/shard_map/ppermute | solution.py:114
  233.5 2.8 collective-permute-start.73
  237.0 3.0 collective-permute-start.76
  240.0 3.9 %fusion.5 = (f32[729,3]{0,1:T(4,128)S(1)}, f32[729,3]{0,1:T(4,128)S(1)}, f32[729,3]{0,1:T(4,128)S(1)}, f32[729,3]{0,1:T(4,128)S(1)}, f32[729,3]{0,1:T(4,128)S(1)}, /*index=5*/f32[729,3]{0,1:T(4,128)S(1)}) fusion(f32[729,729]{1,0:T(8,128)S(1)} %get-tuple-element.151, f32[729,3]{0,1:T(4,128)S(1)} %collective-permute-done.54, ...), kind=kLoop, calls=%fused_computation.40 | loop fusion | flops 19118754 | bytes 6464772 | tf_op jit(solution)/shard_map/reduce_sum | solution.py:110
  244.1 4.8 %collective-permute-start.66 = (f32[729,3]{0,1:T(4,128)S(1)}, f32[729,3]{0,1:T(4,128)S(1)}, u32[]{:S(2)}, u32[]{:S(2)}) collective-permute-start(f32[729,3]{0,1:T(4,128)S(1)} %neg.53), channel_id=1, source_target_pairs={{0,7},{1,4},{2,5},{3,6},{4,3},{5,0},{6,1},{7,2},{8,15},{9,12},{10,... | collective-permute-start | bytes 26252 | tf_op jit(solution)/shard_map/ppermute | solution.py:114
  262.8 39.7 %psum.7 = f32[]{:T(128)} all-reduce(f32[]{:T(128)S(6)} %add.508), channel_id=1, replica_groups=mesh['z'=4,'y'=2,'x'=4] {'z','y','x'}, use_global_device_ids=true, to_apply=%region_60.61 | all-reduce | flops 1 | bytes 8 | tf_op jit(solution)/shard_map/psum | solution.py:115
  (291 shorter events, 93.5 us)
Async XLA Ops:
  10.6 20.1 %collective-permute-start.32 = (s32[7]{0:T(128)S(1)}, s32[7]{0:T(128)S(1)}, u32[]{:S(2)}, u32[]{:S(2)}) collective-permute-start(s32[7]{0:T(128)S(1)} %get-tuple-element.199), channel_id=1, source_target_pairs={{0,31},{1,28},{2,29},{3,30},{4,27},{5,24},{6,25},{7,26},{8,7},{9,4... | collective-permute-start | bytes 92 | tf_op jit(solution)/shard_map/ppermute | solution.py:71
  17.1 15.2 %collective-permute-start.31 = (s32[7]{0:T(128)S(1)}, s32[7]{0:T(128)S(1)}, u32[]{:S(2)}, u32[]{:S(2)}) collective-permute-start(s32[7]{0:T(128)S(1)} %get-tuple-element.200), channel_id=1, source_target_pairs={{0,25},{1,26},{2,27},{3,24},{4,29},{5,30},{6,31},{7,28},{8,1},{9,2... | collective-permute-start | bytes 92 | tf_op jit(solution)/shard_map/ppermute | solution.py:71
  17.1 17.0 %collective-permute-start.30 = (s32[7]{0:T(128)S(1)}, s32[7]{0:T(128)S(1)}, u32[]{:S(2)}, u32[]{:S(2)}) collective-permute-start(s32[7]{0:T(128)S(1)} %get-tuple-element.201), channel_id=1, source_target_pairs={{0,24},{1,25},{2,26},{3,27},{4,28},{5,29},{6,30},{7,31},{8,0},{9,1... | collective-permute-start | bytes 92 | tf_op jit(solution)/shard_map/ppermute | solution.py:71
  17.6 17.4 %collective-permute-start.29 = (s32[7]{0:T(128)S(1)}, s32[7]{0:T(128)S(1)}, u32[]{:S(2)}, u32[]{:S(2)}) collective-permute-start(s32[7]{0:T(128)S(1)} %get-tuple-element.202), channel_id=1, source_target_pairs={{0,27},{1,24},{2,25},{3,26},{4,31},{5,28},{6,29},{7,30},{8,3},{9,0... | collective-permute-start | bytes 92 | tf_op jit(solution)/shard_map/ppermute | solution.py:71
  18.8 18.0 %collective-permute-start.28 = (s32[7]{0:T(128)S(1)}, s32[7]{0:T(128)S(1)}, u32[]{:S(2)}, u32[]{:S(2)}) collective-permute-start(s32[7]{0:T(128)S(1)} %get-tuple-element.203), channel_id=1, source_target_pairs={{0,29},{1,30},{2,31},{3,28},{4,25},{5,26},{6,27},{7,24},{8,5},{9,6... | collective-permute-start | bytes 92 | tf_op jit(solution)/shard_map/ppermute | solution.py:71
  39.0 10.4 %collective-permute-start.47 = (s32[7]{0:T(128)S(1)}, s32[7]{0:T(128)S(1)}, u32[]{:S(2)}, u32[]{:S(2)}) collective-permute-start(s32[7]{0:T(128)S(1)} %get-tuple-element.184), channel_id=1, source_target_pairs={{0,8},{1,9},{2,10},{3,11},{4,12},{5,13},{6,14},{7,15},{8,16},{9,17... | collective-permute-start | bytes 92 | tf_op jit(solution)/shard_map/ppermute | solution.py:71
  72.6 9.9 %collective-permute-start.17 = (f32[7,7]{1,0:T(8,128)S(1)}, f32[7,7]{1,0:T(8,128)S(1)}, u32[]{:S(2)}, u32[]{:S(2)}) collective-permute-start(f32[7,7]{1,0:T(8,128)S(1)} %bitcast.121), channel_id=1, source_target_pairs={{0,15},{1,12},{2,13},{3,14},{4,11},{5,8},{6,9},{7,10},{8,23},{9,20... | collective-permute-start | bytes 596 | tf_op jit(solution)/shard_map/ppermute | solution.py:70
  77.7 10.7 %collective-permute-start.20 = (f32[7,7]{1,0:T(8,128)S(1)}, f32[7,7]{1,0:T(8,128)S(1)}, u32[]{:S(2)}, u32[]{:S(2)}) collective-permute-start(f32[7,7]{1,0:T(8,128)S(1)} %bitcast.118), channel_id=1, source_target_pairs={{0,11},{1,8},{2,9},{3,10},{4,15},{5,12},{6,13},{7,14},{8,19},{9,16... | collective-permute-start | bytes 596 | tf_op jit(solution)/shard_map/ppermute | solution.py:70
  82.6 11.2 %collective-permute-start.23 = (f32[7,7]{1,0:T(8,128)S(1)}, f32[7,7]{1,0:T(8,128)S(1)}, u32[]{:S(2)}, u32[]{:S(2)}) collective-permute-start(f32[7,7]{1,0:T(8,128)S(1)} %bitcast.115), channel_id=1, source_target_pairs={{0,15},{1,12},{2,13},{3,14},{4,11},{5,8},{6,9},{7,10},{8,23},{9,20... | collective-permute-start | bytes 596 | tf_op jit(solution)/shard_map/ppermute | solution.py:70
  122.1 11.7 %collective-permute-start.53 = (f32[729,3]{0,1:T(4,128)S(1)}, f32[729,3]{0,1:T(4,128)S(1)}, u32[]{:S(2)}, u32[]{:S(2)}) collective-permute-start(f32[729,3]{0,1:T(4,128)S(1)} %get-tuple-element.218), channel_id=1, source_target_pairs={{0,5},{1,6},{2,7},{3,4},{4,1},{5,2},{6,3},{7,0},{8,13},{9,14},{10,... | collective-permute-start | bytes 26252 | tf_op jit(solution)/shard_map/ppermute | solution.py:101
  124.6 12.7 %collective-permute-start.64 = (f32[729,3]{0,1:T(4,128)S(1)}, f32[729,3]{0,1:T(4,128)S(1)}, u32[]{:S(2)}, u32[]{:S(2)}) collective-permute-start(f32[729,3]{0,1:T(4,128)S(1)} %get-tuple-element.207), channel_id=1, source_target_pairs={{0,31},{1,28},{2,29},{3,30},{4,27},{5,24},{6,25},{7,26},{8,7},{9,4... | collective-permute-start | bytes 26252 | tf_op jit(solution)/shard_map/ppermute | solution.py:101
  129.4 10.9 %collective-permute-start.61 = (f32[729,3]{0,1:T(4,128)S(1)}, f32[729,3]{0,1:T(4,128)S(1)}, u32[]{:S(2)}, u32[]{:S(2)}) collective-permute-start(f32[729,3]{0,1:T(4,128)S(1)} %get-tuple-element.210), channel_id=1, source_target_pairs={{0,27},{1,24},{2,25},{3,26},{4,31},{5,28},{6,29},{7,30},{8,3},{9,0... | collective-permute-start | bytes 26252 | tf_op jit(solution)/shard_map/ppermute | solution.py:101
  133.8 13.2 %collective-permute-start.60 = (f32[729,3]{0,1:T(4,128)S(1)}, f32[729,3]{0,1:T(4,128)S(1)}, u32[]{:S(2)}, u32[]{:S(2)}) collective-permute-start(f32[729,3]{0,1:T(4,128)S(1)} %get-tuple-element.211), channel_id=1, source_target_pairs={{0,24},{1,25},{2,26},{3,27},{4,28},{5,29},{6,30},{7,31},{8,0},{9,1... | collective-permute-start | bytes 26252 | tf_op jit(solution)/shard_map/ppermute | solution.py:101
  172.7 63.7 %collective-permute-start.65 = (f32[729,3]{0,1:T(4,128)S(1)}, f32[729,3]{0,1:T(4,128)S(1)}, u32[]{:S(2)}, u32[]{:S(2)}) collective-permute-start(f32[729,3]{0,1:T(4,128)S(1)} %neg.52), channel_id=1, source_target_pairs={{0,1},{1,2},{2,3},{3,0},{4,5},{5,6},{6,7},{7,4},{8,9},{9,10},{10,1... | collective-permute-start | bytes 26252 | tf_op jit(solution)/shard_map/ppermute | solution.py:114
  229.9 14.1 %collective-permute-start.72 = (f32[729,3]{0,1:T(4,128)S(1)}, f32[729,3]{0,1:T(4,128)S(1)}, u32[]{:S(2)}, u32[]{:S(2)}) collective-permute-start(f32[729,3]{0,1:T(4,128)S(1)} %neg.59), channel_id=1, source_target_pairs={{0,11},{1,8},{2,9},{3,10},{4,15},{5,12},{6,13},{7,14},{8,19},{9,16... | collective-permute-start | bytes 26252 | tf_op jit(solution)/shard_map/ppermute | solution.py:114
  233.5 10.6 %collective-permute-start.73 = (f32[729,3]{0,1:T(4,128)S(1)}, f32[729,3]{0,1:T(4,128)S(1)}, u32[]{:S(2)}, u32[]{:S(2)}) collective-permute-start(f32[729,3]{0,1:T(4,128)S(1)} %neg.60), channel_id=1, source_target_pairs={{0,8},{1,9},{2,10},{3,11},{4,12},{5,13},{6,14},{7,15},{8,16},{9,17... | collective-permute-start | bytes 26252 | tf_op jit(solution)/shard_map/ppermute | solution.py:114
  236.4 12.6 %collective-permute-start.74 = (f32[729,3]{0,1:T(4,128)S(1)}, f32[729,3]{0,1:T(4,128)S(1)}, u32[]{:S(2)}, u32[]{:S(2)}) collective-permute-start(f32[729,3]{0,1:T(4,128)S(1)} %neg.61), channel_id=1, source_target_pairs={{0,9},{1,10},{2,11},{3,8},{4,13},{5,14},{6,15},{7,12},{8,17},{9,18... | collective-permute-start | bytes 26252 | tf_op jit(solution)/shard_map/ppermute | solution.py:114
  236.4 12.6 %collective-permute-start.75 = (f32[729,3]{0,1:T(4,128)S(1)}, f32[729,3]{0,1:T(4,128)S(1)}, u32[]{:S(2)}, u32[]{:S(2)}) collective-permute-start(f32[729,3]{0,1:T(4,128)S(1)} %neg.62), channel_id=1, source_target_pairs={{0,15},{1,12},{2,13},{3,14},{4,11},{5,8},{6,9},{7,10},{8,23},{9,20... | collective-permute-start | bytes 26252 | tf_op jit(solution)/shard_map/ppermute | solution.py:114
  237.0 14.0 %collective-permute-start.76 = (f32[729,3]{0,1:T(4,128)S(1)}, f32[729,3]{0,1:T(4,128)S(1)}, u32[]{:S(2)}, u32[]{:S(2)}) collective-permute-start(f32[729,3]{0,1:T(4,128)S(1)} %neg.63), channel_id=1, source_target_pairs={{0,12},{1,13},{2,14},{3,15},{4,8},{5,9},{6,10},{7,11},{8,20},{9,21... | collective-permute-start | bytes 26252 | tf_op jit(solution)/shard_map/ppermute | solution.py:114
  244.0 58.5 %collective-permute-start.77 = (f32[729,3]{0,1:T(4,128)S(1)}, f32[729,3]{0,1:T(4,128)S(1)}, u32[]{:S(2)}, u32[]{:S(2)}) collective-permute-start(f32[729,3]{0,1:T(4,128)S(1)} %neg.64), channel_id=1, source_target_pairs={{0,13},{1,14},{2,15},{3,12},{4,9},{5,10},{6,11},{7,8},{8,21},{9,22... | collective-permute-start | bytes 26252 | tf_op jit(solution)/shard_map/ppermute | solution.py:114
  244.1 58.4 %collective-permute-start.66 = (f32[729,3]{0,1:T(4,128)S(1)}, f32[729,3]{0,1:T(4,128)S(1)}, u32[]{:S(2)}, u32[]{:S(2)}) collective-permute-start(f32[729,3]{0,1:T(4,128)S(1)} %neg.53), channel_id=1, source_target_pairs={{0,7},{1,4},{2,5},{3,6},{4,3},{5,0},{6,1},{7,2},{8,15},{9,12},{10,... | collective-permute-start | bytes 26252 | tf_op jit(solution)/shard_map/ppermute | solution.py:114
  248.9 53.6 %collective-permute-start.68 = (f32[729,3]{0,1:T(4,128)S(1)}, f32[729,3]{0,1:T(4,128)S(1)}, u32[]{:S(2)}, u32[]{:S(2)}) collective-permute-start(f32[729,3]{0,1:T(4,128)S(1)} %neg.55), channel_id=1, source_target_pairs={{0,5},{1,6},{2,7},{3,4},{4,1},{5,2},{6,3},{7,0},{8,13},{9,14},{10,... | collective-permute-start | bytes 26252 | tf_op jit(solution)/shard_map/ppermute | solution.py:114
  249.0 53.5 %collective-permute-start.69 = (f32[729,3]{0,1:T(4,128)S(1)}, f32[729,3]{0,1:T(4,128)S(1)}, u32[]{:S(2)}, u32[]{:S(2)}) collective-permute-start(f32[729,3]{0,1:T(4,128)S(1)} %neg.56), channel_id=1, source_target_pairs={{0,15},{1,12},{2,13},{3,14},{4,11},{5,8},{6,9},{7,10},{8,23},{9,20... | collective-permute-start | bytes 26252 | tf_op jit(solution)/shard_map/ppermute | solution.py:114
  251.0 51.5 %collective-permute-start.67 = (f32[729,3]{0,1:T(4,128)S(1)}, f32[729,3]{0,1:T(4,128)S(1)}, u32[]{:S(2)}, u32[]{:S(2)}) collective-permute-start(f32[729,3]{0,1:T(4,128)S(1)} %neg.54), channel_id=1, source_target_pairs={{0,4},{1,5},{2,6},{3,7},{4,0},{5,1},{6,2},{7,3},{8,12},{9,13},{10,... | collective-permute-start | bytes 26252 | tf_op jit(solution)/shard_map/ppermute | solution.py:114
  (56 other events, 526.0 us)
where the time goes:
time: 304 us; the launch traced here: 303 us
  starting transfers between devices  121 us (40%)
  other arithmetic  105 us (35%)
  blocking collectives  39.7 us (13%)
  local copies, waits for them, and re-layouts  22.1 us (7%)
  between operations  13.9 us (5%)
    reduce_sum x1, other arithmetic, pair_block(): return (f_scale[:, :, None] * delta_r, jnp.sum(pair_energy))  42.5 us
    reduce_sum x3, other arithmetic, local_step(): force_sum = force_sum + jnp.sum(pair_force, axis=1)  41 us
    ppermute x26, starting transfers between devices, local_step(): arrived_id.append(lax.ppermute(packet_id[dir_index], MESH_AXES, perm_pairs))  40.4 us
    psum x1, blocking collectives, local_step(): energy = lax.psum(energy_sum, MESH_AXES)  39.7 us
    ppermute x26, starting transfers between devices, local_step(): arrived.append(lax.ppermute(packet[dir_index], MESH_AXES, perm_pairs))  39.5 us
    ppermute x13, starting transfers between devices, local_step(): lax.ppermute(reactions[dir_index], MESH_AXES, shift_perm(mesh_sizes, dire...  20.6 us
    ppermute x13, starting transfers between devices, local_step(): lax.ppermute(ghost_out, MESH_AXES, shift_perm(mesh_sizes, back_dir))  20.1 us
  transfers between devices with their start and end apart: 78, of which 2 were waited for; matrix products, arithmetic and copies ran while one was open for 25% of the time, Pallas kernels for 0%

commit v1 on v0

v1 whole, which is shorter than its diff:
```python
import functools

import jax
import jax.numpy as jnp
from jax import lax
from jax.experimental import pallas as pl
from jax.experimental.pallas import tpu as pltpu
from jax.sharding import PartitionSpec as P

DT = 0.005
RC = 2.5
FAR = 1.0e6
UCUT = 4.0 * (RC ** -12 - RC ** -6)
UPC = -48.0 * RC ** -13 + 24.0 * RC ** -7
MESH_AXES = ("z", "y", "x")
DIRS = [(dx, dy, dz) for dz in (-1, 0, 1) for dy in (-1, 0, 1) for dx in (-1, 0, 1) if (dx, dy, dz) != (0, 0, 0)]
NEAR = RC + 1.0e-3
PACK = 8
L = 128
F32 = jnp.float32
BF16 = jnp.bfloat16
I32 = jnp.int32
NT = (((1,), (1,)), ((), ()))
NN = (((1,), (0,)), ((), ()))


def order_of(d):
    if d[2] == 0:
        return 1 if d[1] != 0 else 2
    return 2 if (d[1] == 0 and d[0] != 0) else 0


def range_of(d):
    cx, cy, cz = [(1, 0, 2)[c] for c in (d[0], d[1], d[2])]
    kind = order_of(d)
    if kind == 0:
        if d[0] == 0 and d[1] == 0:
            return cz * 9, cz * 9 + 9
        if d[0] == 0:
            return cz * 9 + cy * 3, cz * 9 + cy * 3 + 3
        return cz * 9 + cy * 3 + cx, cz * 9 + cy * 3 + cx + 1
    if kind == 1:
        if d[0] == 0:
            return cy * 9, cy * 9 + 9
        return cy * 9 + cx * 3, cy * 9 + cx * 3 + 3
    if d[2] == 0:
        return cx * 9, cx * 9 + 9
    return cx * 9 + cz * 3, cx * 9 + cz * 3 + 3


def split3(x):
    hi = x.astype(BF16)
    rest = x - hi.astype(F32)
    mid = rest.astype(BF16)
    low = (rest - mid.astype(F32)).astype(BF16)
    return hi, mid, low


def onehot_rows(dest, base, count):
    rows = lax.broadcasted_iota(I32, (count, dest.shape[1]), 0) + base
    return jnp.where(rows == dest, 1.0, 0.0).astype(BF16)


def scatter_lanes(data, dest, slots):
    rows = data.shape[0]
    parts = jnp.concatenate(split3(data), axis=0)
    out = []
    for base in range(0, slots, 256):
        hot = onehot_rows(dest, base, min(256, slots - base))
        got = lax.dot_general(parts, hot, NT, preferred_element_type=F32)
        out.append(got[0:rows] + got[rows:2 * rows] + got[2 * rows:3 * rows])
    return jnp.concatenate(out, axis=1)


def class_places(code, with_before):
    width = code.shape[1]
    tiles = width // L
    cls = lax.broadcasted_iota(I32, (32, width), 0)
    member = jnp.where(cls == code, 1.0, 0.0)
    member_b = member.astype(BF16)
    stacked = jnp.concatenate([member_b[:, t * L:(t + 1) * L] for t in range(tiles)], axis=0)
    row_i = lax.broadcasted_iota(I32, (L, 256), 0)
    col_i = lax.broadcasted_iota(I32, (L, 256), 1)
    tri = jnp.where((row_i < col_i) | (col_i >= L), 1.0, 0.0).astype(BF16)
    pre = lax.dot_general(stacked, tri, NN, preferred_element_type=F32)
    carry = jnp.zeros((32, L), F32)
    if with_before:
        before_b = jnp.where(code < cls, 1.0, 0.0).astype(BF16)
        before_s = before_b[:, 0:L]
        tot = None
        ones = jnp.ones((L, L), BF16)
        for t in range(tiles):
            part = lax.dot_general(before_b[:, t * L:(t + 1) * L], ones, NN, preferred_element_type=F32)
            tot = part if tot is None else tot + part
        before = tot
        carry = before
    else:
        before = None
    places = []
    for t in range(tiles):
        within = pre[32 * t:32 * t + 32, 0:L] + carry
        places.append(jnp.sum(member[:, t * L:(t + 1) * L] * within, axis=0, keepdims=True))
        carry = carry + pre[32 * t:32 * t + 32, L:256]
    return jnp.concatenate(places, axis=1), before


def pad_lanes(x, width):
    return jnp.concatenate([x, jnp.zeros((x.shape[0], width - x.shape[1]), x.dtype)], axis=1)


def exchange_kernel(sizes, peers, slots, pos_ref, vel_ref, frc_ref, id_ref, ok_ref, side_ref, srt_ref, gh_ref, pkt, rcv, out3, psend, precv, gsend, grecv):
    size_x, size_y, size_z = sizes
    me = (lax.axis_index("x"), lax.axis_index("y"), lax.axis_index("z"))

    def device_at(offset):
        return (lax.rem(me[2] + offset[2], size_z), lax.rem(me[1] + offset[1], size_y), lax.rem(me[0] + offset[0], size_x))

    barrier = pltpu.get_barrier_semaphore()
    for offset in peers:
        pl.semaphore_signal(barrier, inc=1, device_id=device_at(offset), device_id_type=pl.DeviceIdType.MESH)

    n = pos_ref.shape[1]
    side = side_ref[0, 0]
    owned = pad_lanes(ok_ref[...], slots) > 0
    half = vel_ref[...] + (0.5 * DT) * frc_ref[...]
    free = pos_ref[...] + DT * half
    half = pad_lanes(half, slots)
    free = pad_lanes(free, slots)
    ids = pad_lanes(id_ref[...], slots)
    code = jnp.zeros((1, slots), I32)
    moved = []
    low_side = []
    for axis in range(3):
        low = me[axis].astype(F32) * side
        high = (me[axis] + 1).astype(F32) * side
        box = side * float(sizes[axis])
        u = free[axis:axis + 1]
        step = jnp.where(u >= high, 1, 0) - jnp.where(u < low, 1, 0)
        code = code + (step + 1) * (1, 3, 9)[axis]
        moved.append(jnp.where(u < 0.0, u + box, jnp.where(u >= box, u - box, u)))
        low_side.append(low)
    code = jnp.where(owned, code, 31)
    id_hi = (ids >> 16).astype(F32)
    id_lo = (ids & 65535).astype(F32)
    okf = jnp.where(owned, 1.0, 0.0)
    data = jnp.concatenate(moved + [half, id_hi, id_lo, okf, jnp.zeros((7, slots), F32)], axis=0)

    place, _ = class_places(code, False)
    leaving = owned & (code != 13)
    target = jnp.where(leaving, (code - jnp.where(code > 13, 1, 0)) * PACK + place.astype(I32), -1)
    hot = onehot_rows(target, 0, 26 * PACK)
    parts = split3(data)
    got = lax.dot_general(hot, parts[0], NT, preferred_element_type=F32)
    got = got + lax.dot_general(hot, parts[1], NT, preferred_element_type=F32)
    got = got + lax.dot_general(hot, parts[2], NT, preferred_element_type=F32)
    pkt[...] = jnp.concatenate([got, jnp.zeros((26 * PACK, 112), F32)], axis=1)

    pl.semaphore_wait(barrier, len(peers))
    copies = []
    for index, d in enumerate(DIRS):
        offset = (d[0] % size_x, d[1] % size_y, d[2] % size_z)
        copy = pltpu.make_async_remote_copy(
            src_ref=pkt.at[pl.ds(index * PACK, PACK)], dst_ref=rcv.at[pl.ds(index * PACK, PACK)],
            send_sem=psend.at[index], recv_sem=precv.at[index],
            device_id=device_at(offset), device_id_type=pl.DeviceIdType.MESH)
        copy.start()
        copies.append(copy)
    staying = code == 13
    stay_f = jnp.where(staying, 1.0, 0.0)
    for copy in copies:
        copy.wait_recv()

    came = jnp.concatenate([rcv[...], jnp.zeros((256 - 26 * PACK, L), F32)], axis=0)
    came_t = jnp.transpose(came)[0:16]
    valid = jnp.concatenate([staying, came_t[8:9] > 0.5], axis=1)
    cand = jnp.concatenate([data, came_t], axis=1)
    bins = []
    for axis in range(3):
        loc = cand[axis:axis + 1] - low_side[axis]
        bins.append(jnp.where(loc < NEAR, 0, jnp.where(loc > side - NEAR, 2, 1)))
    cx, cy, cz = bins
    orders = [cz * 9 + cy * 3 + cx, cy * 9 + cx * 3 + cz, cx * 9 + cz * 3 + cy]
    lane = lax.broadcasted_iota(I32, (1, slots), 1).astype(F32)
    eye = lax.broadcasted_iota(I32, (32, L), 0) == lax.broadcasted_iota(I32, (32, L), 1)
    cand8 = cand[0:8]
    gcopies = []
    for kind in range(3):
        key = jnp.where(valid, orders[kind], 28)
        place, before = class_places(key, True)
        dest = jnp.where(valid, place.astype(I32), -1)
        arranged = scatter_lanes(cand8, dest, slots)
        total = jnp.concatenate([before[27:28]] * (slots // L), axis=1)
        xyz = jnp.where(lane < total, arranged[0:3], FAR)
        counts = jnp.sum(jnp.where(eye, before, 0.0), axis=0, keepdims=True)
        out3[kind] = jnp.concatenate([xyz, pad_lanes(counts, slots)], axis=0)
        for index, offset in enumerate(peers):
            sign = tuple(0 if c == 0 else 1 for c in offset)
            if order_of(sign) != kind:
                continue
            copy = pltpu.make_async_remote_copy(
                src_ref=out3.at[kind], dst_ref=gh_ref.at[index],
                send_sem=gsend.at[index], recv_sem=grecv.at[index],
                device_id=device_at(offset), device_id_type=pl.DeviceIdType.MESH)
            copy.start()
            gcopies.append(copy)

    arr_ids = came[:, 6:7].astype(I32) * 65536 + came[:, 7:8].astype(I32)
    arr_ok = came[:, 8:9] > 0.5
    row_ids = jnp.concatenate([ids, came_t[6:7].astype(I32) * 65536 + came_t[7:8].astype(I32)], axis=1)
    less = jnp.where((arr_ids < row_ids) & arr_ok, 1.0, 0.0)
    arrivals_below = jnp.sum(less, axis=0, keepdims=True)
    above = jnp.where((arr_ids > row_ids[:, 0:slots]) & staying, 1.0, 0.0).astype(BF16)
    stay_below = lax.dot_general(jnp.ones((16, slots), BF16), above, NT, preferred_element_type=F32)[0:1]
    stay_place, _ = class_places(jnp.where(staying, 0, 31), False)
    rank = jnp.concatenate([stay_place, stay_below], axis=1) + arrivals_below
    dest = jnp.where(valid, rank.astype(I32), -1)
    srt_ref[...] = scatter_lanes(cand, dest, slots)

    for copy in gcopies:
        copy.wait_recv()
    for copy in copies + gcopies:
        copy.wait_send()


def force_kernel(sizes, peers, slots, unroll, srt_ref, gh_ref, offs_ref, side_ref, pos_ref, vel_ref, frc_ref, id_ref, ok_ref, en_ref, rolled, cols, acc):
    size_x, size_y, size_z = sizes
    me = (lax.axis_index("x"), lax.axis_index("y"), lax.axis_index("z"))
    n = pos_ref.shape[1]
    side = side_ref[0, 0]
    tiles = slots // L
    okrow = srt_ref[8:9]
    own = jnp.where(okrow > 0.5, srt_ref[0:3], -FAR)
    count = jnp.sum(okrow).astype(I32)
    wide = side > 2.0 * NEAR

    def put(block, length, start):
        rolled[...] = block

        def one(t, carry):
            tile = rolled[:, pl.ds(pl.multiple_of(t * L, L), L)]
            cols[pl.ds(pl.multiple_of(start + t * L, 8), L), 0:8] = jnp.transpose(tile)
            return carry

        lax.fori_loop(0, (length + 127) // L, one, 0)
        return start + ((length + 7) // 8) * 8

    pad5 = jnp.zeros((5, slots), F32)
    fill = put(jnp.concatenate([jnp.where(okrow > 0.5, srt_ref[0:3], FAR), pad5], axis=0), count, jnp.int32(0))
    for d in DIRS:
        offset = (d[0] % size_x, d[1] % size_y, d[2] % size_z)
        back = ((-offset[0]) % size_x, (-offset[1]) % size_y, (-offset[2]) % size_z)
        index = peers.index(back)
        first, last = range_of(d)
        begin = jnp.where(wide, offs_ref[index, first], 0)
        end = jnp.where(wide, offs_ref[index, last], offs_ref[index, 27])
        shifts = []
        for axis in range(3):
            box = side * float(sizes[axis])
            if d[axis] == 1:
                shifts.append(jnp.where(me[axis] == sizes[axis] - 1, box, 0.0))
            elif d[axis] == -1:
                shifts.append(jnp.where(me[axis] == 0, -box, 0.0))
            else:
                shifts.append(jnp.float32(0.0))
        block = jnp.concatenate([gh_ref[index, a:a + 1] + shifts[a] for a in range(3)] + [pad5], axis=0)
        block = pltpu.roll(block, lax.rem(slots - begin, slots), 1)
        fill = put(block, end - begin, fill)
    cols[pl.ds(pl.multiple_of(fill, 8), 8 * unroll), 0:8] = jnp.full((8 * unroll, 8), FAR, F32)
    steps = (fill // 8 + unroll - 1) // unroll

    def sweep(used):
        ox, oy, oz = [[jnp.broadcast_to(own[a:a + 1, t * L:t * L + L], (8, L)) for t in range(used)] for a in range(3)]

        def body(i, carry):
            fx, fy, fz, en = [list(c) for c in carry]
            for u in range(unroll):
                col = cols[pl.ds(pl.multiple_of((i * unroll + u) * 8, 8), 8), :]
                gx = jnp.broadcast_to(col[:, 0:1], (8, L))
                gy = jnp.broadcast_to(col[:, 1:2], (8, L))
                gz = jnp.broadcast_to(col[:, 2:3], (8, L))
                for t in range(used):
                    dx = ox[t] - gx
                    dy = oy[t] - gy
                    dz = oz[t] - gz
                    d2 = dx * dx + dy * dy + dz * dz
                    near = (d2 < RC * RC) & (d2 > 0.0)
                    inv = lax.rsqrt(d2)
                    inv2 = inv * inv
                    inv6 = inv2 * inv2 * inv2
                    scale = jnp.where(near, (48.0 * inv6 - 24.0) * inv6 * inv2 + UPC * inv, 0.0)
                    pair = jnp.where(near, (4.0 * inv6 - 4.0) * inv6 + (RC * UPC - UCUT) - UPC * (d2 * inv), 0.0)
                    fx[t] = fx[t] + scale * dx
                    fy[t] = fy[t] + scale * dy
                    fz[t] = fz[t] + scale * dz
                    en[t] = en[t] + pair
            return tuple(fx), tuple(fy), tuple(fz), tuple(en)

        zero = tuple(jnp.zeros((8, L), F32) for _ in range(used))
        sums = lax.fori_loop(0, steps, body, (zero,) * 4)
        for a in range(4):
            for t in range(used):
                acc[a:a + 1, t * L:t * L + L] = jnp.sum(sums[a][t], axis=0, keepdims=True)

    acc[...] = jnp.zeros_like(acc)
    need = (count + 127) // L
    for used in range(1, tiles + 1):
        if used <= 3:
            if used == 3:
                pl.when(need <= 3)(functools.partial(sweep, used))
        else:
            pl.when(need == used)(functools.partial(sweep, used))

    force = acc[0:3] * okrow
    pos_ref[...] = srt_ref[0:3, 0:n]
    frc_ref[...] = force[:, 0:n]
    vel_ref[...] = ((srt_ref[3:6] + (0.5 * DT) * force) * okrow)[:, 0:n]
    id_ref[...] = (srt_ref[6:7].astype(I32) * 65536 + srt_ref[7:8].astype(I32))[:, 0:n]
    ok_ref[...] = okrow[:, 0:n].astype(I32)
    en_ref[0, 0] = 0.5 * jnp.sum(acc[3:4] * okrow)


def solution(mesh):
    sizes = (mesh.shape["x"], mesh.shape["y"], mesh.shape["z"])
    peers = sorted({(d[0] % sizes[0], d[1] % sizes[1], d[2] % sizes[2]) for d in DIRS} - {(0, 0, 0)})
    unroll = 2

    def local_step(atom_pos, atom_vel, atom_frc, atom_id, atom_ok, brick_side):
        n = atom_pos.shape[0]
        slots = -(-n // L) * L
        side = jnp.reshape(brick_side, (1, 1))
        vmem = pl.BlockSpec(memory_space=pltpu.VMEM)
        smem = pl.BlockSpec(memory_space=pltpu.SMEM)
        srt, ghosts = pl.pallas_call(
            functools.partial(exchange_kernel, sizes, peers, slots),
            out_shape=(jax.ShapeDtypeStruct((16, slots), F32), jax.ShapeDtypeStruct((len(peers), 4, slots), F32)),
            in_specs=[vmem] * 5 + [smem],
            out_specs=(vmem, vmem),
            scratch_shapes=[
                pltpu.VMEM((26 * PACK, L), F32), pltpu.VMEM((26 * PACK, L), F32), pltpu.VMEM((3, 4, slots), F32),
                pltpu.SemaphoreType.DMA((26,)), pltpu.SemaphoreType.DMA((26,)),
                pltpu.SemaphoreType.DMA((len(peers),)), pltpu.SemaphoreType.DMA((len(peers),)),
            ],
            compiler_params=pltpu.CompilerParams(collective_id=0, has_side_effects=True, vmem_limit_bytes=40 * 2 ** 20),
            name="exchange",
        )(atom_pos.T, atom_vel.T, atom_frc.T, atom_id[None, :], atom_ok[None, :], side)
        offs = ghosts[:, 3, 0:32].astype(I32)
        out_f = jax.ShapeDtypeStruct((3, n), F32)
        out_i = jax.ShapeDtypeStruct((1, n), I32)
        new_pos, new_vel, new_frc, new_id, new_ok, energy = pl.pallas_call(
            functools.partial(force_kernel, sizes, peers, slots, unroll),
            out_shape=(out_f, out_f, out_f, out_i, out_i, jax.ShapeDtypeStruct((1, 1), F32)),
            in_specs=[vmem, vmem, smem, smem],
            out_specs=(vmem, vmem, vmem, vmem, vmem, smem),
            scratch_shapes=[pltpu.VMEM((8, slots), F32), pltpu.VMEM((27 * slots + L + 8 * unroll, L), F32), pltpu.VMEM((4, slots), F32)],
            compiler_params=pltpu.CompilerParams(vmem_limit_bytes=40 * 2 ** 20),
            name="forces",
        )(srt, ghosts, offs, side)
        energy = lax.psum(energy[0, 0], MESH_AXES)
        return new_pos.T, new_vel.T, new_frc.T, new_id[0], new_ok[0], energy

    row_spec = P(MESH_AXES, None)
    id_spec = P(MESH_AXES)
    return jax.shard_map(local_step, mesh=mesh, in_specs=(row_spec, row_spec, row_spec, id_spec, id_spec, P()), out_specs=(row_spec, row_spec, row_spec, id_spec, id_spec, P()), check_vma=False)
```

time: 304 us -> 82.3 us (0.27)
  starting transfers between devices: 121 us -> 0 us
  other arithmetic: 105 us -> 1.22 us
  Pallas kernels: 0 us -> 35.8 us
  local copies, waits for them, and re-layouts: 22.1 us -> 2.14 us
  between operations: 13.9 us -> 1.35 us
    ppermute x78 -> x0, starting transfers between devices: 121 us -> none  [the longest x26 40.4 us: local_step(): arrived_id.append(lax.ppermute(packet_id[dir_index], MESH_AXES, perm_pairs))]
    reduce_sum x6 -> x0, other arithmetic: 86 us -> none  [the longest x1 42.5 us: pair_block(): return (f_scale[:, :, None] * delta_r, jnp.sum(pair_energy))]
    pallas_call x0 -> x2, Pallas kernels: none -> 35.8 us  [the longest x1 18.3 us: local_step(): pl.pallas_call(functools.partial(exchange_kernel, sizes, peers, slots), o...]
    gather x14 -> x0, local copies, waits for them, and re-layouts: 14.9 us -> none  [the longest x1 5 us: local_step(): new_ok = cand_ok[keep_order]]
    select_n x10 -> x0, other arithmetic: 6.33 us -> none  [the longest x1 4.63 us: pair_block(): jnp.where(in_range, (48.0 * inv_r6 * inv_r6 - 24.0 * inv_r6) * inv_r2 + U...]
    sort x1 -> x0, other arithmetic: 4.4 us -> none  [local_step(): keep_order = jnp.argsort(jnp.where(cand_ok, cand_id, 2147483647))[:capacity]]
    slice x31 -> x0, local copies, waits for them, and re-layouts: 3.32 us -> none  [the longest x28 2.47 us: local_step(): arrived.append(lax.ppermute(packet[dir_index], MESH_AXES, perm_pairs))]
  transfers between devices with their start and end apart: 78 -> 0, of which waited for: 2 -> 0; matrix products, arithmetic and copies ran while one was open for 25% -> 0% of each run, Pallas kernels for 0% -> 0%
where the time goes in v1:
time: 82.3 us; the launch traced here: 82.1 us
  blocking collectives  41.6 us (51%)
  Pallas kernels  35.8 us (43%)
  local copies, waits for them, and re-layouts  2.14 us (3%)
  between operations  1.35 us (2%)
  other arithmetic  1.22 us (1%)
    psum x1, blocking collectives, local_step(): energy = lax.psum(energy[0, 0], MESH_AXES)  41.6 us
    pallas_call x1, Pallas kernels, local_step(): pl.pallas_call(functools.partial(exchange_kernel, sizes, peers, slots), o...  18.3 us
    pallas_call x1, Pallas kernels, local_step(): pl.pallas_call(functools.partial(force_kernel, sizes, peers, slots, unrol...  17.5 us

profile of v1, /device:TPU:0, one launch (start us, length us, event | category | flops | bytes accessed | tf_op | source)
XLA Modules:
  0.0 82.1 jit_solution(13631399836650696165)
XLA Ops:
  0.6 0.0 copy-start.1
  1.3 0.0 copy-start
  1.3 0.7 broadcast_in_dim.6.id_ref
  2.0 0.7 broadcast_in_dim.7.ok_ref
  2.7 0.0 copy-done.1
  2.7 0.0 copy-done
  2.7 0.0 copy-start.2
  2.7 0.7 copy-done.2
  3.4 18.3 %exchange.1 = (f32[16,768]{1,0:T(8,128)S(1)}, f32[17,4,768]{2,1,0:T(4,128)S(1)}) custom-call(f32[3,729]{1,0:T(4,128)S(1)} %bitcast.12, f32[3,729]{1,0:T(4,128)S(1)} %bitcast.13, f32[3,729]{1,0:T(4,128)S(1)} %bitcast.14, s32[1,729]{1,0:T(1,128)S(1)} %broadcast_in_dim.6.id_ref, s32[1,729]{1,0:T(1,128)S(1)} %broadcast_in_dim.7.ok_ref, f32[1,1]{1,0:T(1,128)} %bitcast.10.side_ref), custom_call_target="tpu_custom_call" | custom-call | tf_op jit(solution)/shard_map/exchange/pallas_call | solution.py:333
  21.8 17.5 %forces.1 = (f32[3,729]{1,0:T(4,128)}, f32[3,729]{1,0:T(4,128)}, f32[3,729]{1,0:T(4,128)}, s32[1,729]{1,0:T(1,128)S(1)}, s32[1,729]{1,0:T(1,128)S(1)}, /*index=5*/f32[1,1]{1,0:T(1,128)}) custom-call(f32[16,768]{1,0:T(8,128)S(1)} %get-tuple-element.14.srt_ref, f32[17,4,768]{2,1,0:T(4,128)S(1)} %get-tuple-element.15.gh_ref, s32[17,32]{1,0:T(8,128)S(1)} %fusion.offs_ref, ...), custom_call_target="tpu_custom_call" | custom-call | tf_op jit(solution)/shard_map/forces/pallas_call | solution.py:349
  39.3 41.6 %psum.7 = f32[]{:T(128)} all-reduce(f32[]{:T(128)} %bitcast.8), channel_id=1, replica_groups=mesh['z'=4,'y'=2,'x'=4] {'z','y','x'}, use_global_device_ids=true, to_apply=%region_0.0 | all-reduce | flops 1 | bytes 8 | tf_op jit(solution)/shard_map/psum | solution.py:358
  80.8 0.6 reduce
  81.4 0.6 reduce.1
  (2 shorter events, 0.1 us)
Async XLA Ops:
  0.6 2.1 %copy-start.1 = (f32[729,3]{0,1:T(4,128)S(1)}, f32[729,3]{0,1:T(4,128)}, u32[]{:S(2)}) copy-start(f32[729,3]{0,1:T(4,128)} %param.7) | copy-start | bytes 26248
  1.3 1.4 %copy-start = (f32[729,3]{0,1:T(4,128)S(1)}, f32[729,3]{0,1:T(4,128)}, u32[]{:S(2)}) copy-start(f32[729,3]{0,1:T(4,128)} %param.6) | copy-start | bytes 26248
  2.7 0.7 copy-start.2

commit v2 on v1

--- a/solution.py
+++ b/solution.py
@@ -246,6 +246,10 @@
 
     pad5 = jnp.zeros((5, slots), F32)
     fill = put(jnp.concatenate([jnp.where(okrow > 0.5, srt_ref[0:3], FAR), pad5], axis=0), count, jnp.int32(0))
+    spare = jnp.full((8 * unroll, 8), FAR, F32)
+    cols[pl.ds(pl.multiple_of(fill, 8), 8 * unroll), 0:8] = spare
+    self_steps = (fill // 8 + unroll - 1) // unroll
+    fill = self_steps * (8 * unroll)
     for d in DIRS:
         offset = (d[0] % size_x, d[1] % size_y, d[2] % size_z)
         back = ((-offset[0]) % size_x, (-offset[1]) % size_y, (-offset[2]) % size_z)
@@ -265,50 +269,51 @@
         block = jnp.concatenate([gh_ref[index, a:a + 1] + shifts[a] for a in range(3)] + [pad5], axis=0)
         block = pltpu.roll(block, lax.rem(slots - begin, slots), 1)
         fill = put(block, end - begin, fill)
-    cols[pl.ds(pl.multiple_of(fill, 8), 8 * unroll), 0:8] = jnp.full((8 * unroll, 8), FAR, F32)
+    cols[pl.ds(pl.multiple_of(fill, 8), 8 * unroll), 0:8] = spare
     steps = (fill // 8 + unroll - 1) // unroll
 
     def sweep(used):
         ox, oy, oz = [[jnp.broadcast_to(own[a:a + 1, t * L:t * L + L], (8, L)) for t in range(used)] for a in range(3)]
 
-        def body(i, carry):
-            fx, fy, fz, en = [list(c) for c in carry]
+        def body(with_self, i, carry):
+            fx, fy, fz, en = list(carry[0]), list(carry[1]), list(carry[2]), carry[3]
             for u in range(unroll):
                 col = cols[pl.ds(pl.multiple_of((i * unroll + u) * 8, 8), 8), :]
-                gx = jnp.broadcast_to(col[:, 0:1], (8, L))
-                gy = jnp.broadcast_to(col[:, 1:2], (8, L))
-                gz = jnp.broadcast_to(col[:, 2:3], (8, L))
+                gx, gy, gz = [jnp.broadcast_to(col[:, a:a + 1], (8, L)) for a in range(3)]
                 for t in range(used):
                     dx = ox[t] - gx
                     dy = oy[t] - gy
                     dz = oz[t] - gz
                     d2 = dx * dx + dy * dy + dz * dz
-                    near = (d2 < RC * RC) & (d2 > 0.0)
-                    inv = lax.rsqrt(d2)
-                    inv2 = inv * inv
-                    inv6 = inv2 * inv2 * inv2
-                    scale = jnp.where(near, (48.0 * inv6 - 24.0) * inv6 * inv2 + UPC * inv, 0.0)
-                    pair = jnp.where(near, (4.0 * inv6 - 4.0) * inv6 + (RC * UPC - UCUT) - UPC * (d2 * inv), 0.0)
+                    near = d2 < RC * RC
+                    if with_self:
+                        near = near & (d2 > 0.0)
+                    inv = jnp.where(near, lax.rsqrt(d2), 0.0)
+                    s2 = inv * inv
+                    s6 = s2 * s2 * s2
+                    s12 = s6 * s6
+                    p = s12 - s6
+                    w = inv * (UPC / 24.0)
+                    scale = (p + s12) * s2 + w
+                    en = en + ((p + jnp.where(near, 0.25 * (RC * UPC - UCUT), 0.0)) - 6.0 * (w * d2))
                     fx[t] = fx[t] + scale * dx
                     fy[t] = fy[t] + scale * dy
                     fz[t] = fz[t] + scale * dz
-                    en[t] = en[t] + pair
-            return tuple(fx), tuple(fy), tuple(fz), tuple(en)
-
-        zero = tuple(jnp.zeros((8, L), F32) for _ in range(used))
-        sums = lax.fori_loop(0, steps, body, (zero,) * 4)
-        for a in range(4):
+            return tuple(fx), tuple(fy), tuple(fz), en
+
+        zero = jnp.zeros((8, L), F32)
+        sums = lax.fori_loop(0, self_steps, functools.partial(body, True), ((zero,) * used,) * 3 + (zero,))
+        sums = lax.fori_loop(self_steps, steps, functools.partial(body, False), sums)
+        for a in range(3):
             for t in range(used):
-                acc[a:a + 1, t * L:t * L + L] = jnp.sum(sums[a][t], axis=0, keepdims=True)
+                acc[a:a + 1, t * L:t * L + L] = 24.0 * jnp.sum(sums[a][t], axis=0, keepdims=True)
+        en_ref[...] = 2.0 * jnp.sum(sums[3], axis=0, keepdims=True)
 
     acc[...] = jnp.zeros_like(acc)
-    need = (count + 127) // L
-    for used in range(1, tiles + 1):
-        if used <= 3:
-            if used == 3:
-                pl.when(need <= 3)(functools.partial(sweep, used))
-        else:
-            pl.when(need == used)(functools.partial(sweep, used))
+    need = (count + L - 1) // L
+    pl.when(need <= 3)(functools.partial(sweep, min(3, tiles)))
+    for used in range(4, tiles + 1):
+        pl.when(need == used)(functools.partial(sweep, used))
 
     force = acc[0:3] * okrow
     pos_ref[...] = srt_ref[0:3, 0:n]
@@ -316,12 +321,40 @@
     vel_ref[...] = ((srt_ref[3:6] + (0.5 * DT) * force) * okrow)[:, 0:n]
     id_ref[...] = (srt_ref[6:7].astype(I32) * 65536 + srt_ref[7:8].astype(I32))[:, 0:n]
     ok_ref[...] = okrow[:, 0:n].astype(I32)
-    en_ref[0, 0] = 0.5 * jnp.sum(acc[3:4] * okrow)
+
+
+def total_kernel(sizes, part_ref, sum_ref, rows, ssem, rsem):
+    size_x, size_y, size_z = sizes
+    me = (lax.axis_index("x"), lax.axis_index("y"), lax.axis_index("z"))
+    mine = (me[2] * size_y + me[1]) * size_x + me[0]
+    others = [(dx, dy, dz) for dz in range(size_z) for dy in range(size_y) for dx in range(size_x) if dx + dy + dz > 0]
+
+    def device_at(offset):
+        return (lax.rem(me[2] + offset[2], size_z), lax.rem(me[1] + offset[1], size_y), lax.rem(me[0] + offset[0], size_x))
+
+    barrier = pltpu.get_barrier_semaphore()
+    for offset in others:
+        pl.semaphore_signal(barrier, inc=1, device_id=device_at(offset), device_id_type=pl.DeviceIdType.MESH)
+    rows[pl.ds(mine, 1)] = part_ref[...]
+    pl.semaphore_wait(barrier, len(others))
+    copies = []
+    for index, offset in enumerate(others):
+        copy = pltpu.make_async_remote_copy(
+            src_ref=part_ref, dst_ref=rows.at[pl.ds(mine, 1)], send_sem=ssem.at[index], recv_sem=rsem.at[index],
+            device_id=device_at(offset), device_id_type=pl.DeviceIdType.MESH)
+        copy.start()
+        copies.append(copy)
+    for copy in copies:
+        copy.wait_recv()
+    sum_ref[0, 0] = jnp.sum(rows[...])
+    for copy in copies:
+        copy.wait_send()
 
 
 def solution(mesh):
     sizes = (mesh.shape["x"], mesh.shape["y"], mesh.shape["z"])
     peers = sorted({(d[0] % sizes[0], d[1] % sizes[1], d[2] % sizes[2]) for d in DIRS} - {(0, 0, 0)})
+    devices = sizes[0] * sizes[1] * sizes[2]
     unroll = 2
 
     def local_step(atom_pos, atom_vel, atom_frc, atom_id, atom_ok, brick_side):
@@ -348,14 +381,22 @@
         out_i = jax.ShapeDtypeStruct((1, n), I32)
         new_pos, new_vel, new_frc, new_id, new_ok, energy = pl.pallas_call(
             functools.partial(force_kernel, sizes, peers, slots, unroll),
-            out_shape=(out_f, out_f, out_f, out_i, out_i, jax.ShapeDtypeStruct((1, 1), F32)),
+            out_shape=(out_f, out_f, out_f, out_i, out_i, jax.ShapeDtypeStruct((1, L), F32)),
             in_specs=[vmem, vmem, smem, smem],
-            out_specs=(vmem, vmem, vmem, vmem, vmem, smem),
-            scratch_shapes=[pltpu.VMEM((8, slots), F32), pltpu.VMEM((27 * slots + L + 8 * unroll, L), F32), pltpu.VMEM((4, slots), F32)],
+            out_specs=(vmem,) * 6,
+            scratch_shapes=[pltpu.VMEM((8, slots), F32), pltpu.VMEM((27 * slots + L + 8 * unroll, L), F32), pltpu.VMEM((3, slots), F32)],
             compiler_params=pltpu.CompilerParams(vmem_limit_bytes=40 * 2 ** 20),
             name="forces",
         )(srt, ghosts, offs, side)
-        energy = lax.psum(energy[0, 0], MESH_AXES)
+        energy = pl.pallas_call(
+            functools.partial(total_kernel, sizes),
+            out_shape=jax.ShapeDtypeStruct((1, 1), F32),
+            in_specs=[vmem],
+            out_specs=smem,
+            scratch_shapes=[pltpu.VMEM((devices, L), F32), pltpu.SemaphoreType.DMA((devices,)), pltpu.SemaphoreType.DMA((devices,))],
+            compiler_params=pltpu.CompilerParams(collective_id=1, has_side_effects=True),
+            name="total",
+        )(energy)[0, 0]
         return new_pos.T, new_vel.T, new_frc.T, new_id[0], new_ok[0], energy
 
     row_spec = P(MESH_AXES, None)

time: 82.3 us -> 55.7 us (0.68)
  blocking collectives: 41.6 us -> 0 us
  Pallas kernels: 35.8 us -> 48.8 us
  between operations: 1.35 us -> 3.04 us
    psum x1 -> x0, blocking collectives: 41.6 us -> none  [local_step(): energy = lax.psum(energy[0, 0], MESH_AXES)]
    pallas_call x0 -> x1, Pallas kernels: none -> 9.78 us  [local_step(): pl.pallas_call(functools.partial(total_kernel, sizes), out_shape=jax.Shap...]
    pallas_call x1, Pallas kernels: 17.5 us -> 20.8 us  [local_step(): pl.pallas_call(functools.partial(force_kernel, sizes, peers, slots, unrol...]
where the time goes in v2:
time: 55.7 us
  Pallas kernels  48.8 us (88%)
  between operations  3.04 us (5%)
  local copies, waits for them, and re-layouts  2.65 us (5%)
  other arithmetic  1.22 us (2%)
    pallas_call x1, Pallas kernels, local_step(): pl.pallas_call(functools.partial(force_kernel, sizes, peers, slots, unrol...  20.8 us
    pallas_call x1, Pallas kernels, local_step(): pl.pallas_call(functools.partial(exchange_kernel, sizes, peers, slots), o...  18.3 us
    pallas_call x1, Pallas kernels, local_step(): pl.pallas_call(functools.partial(total_kernel, sizes), out_shape=jax.Shap...  9.78 us
    unnamed x8, local copies, waits for them, and re-layouts  1.22 us
    pallas_call x2, other arithmetic, local_step(): pl.pallas_call(functools.partial(force_kernel, sizes, peers, slots, unrol...  1.21 us

profile of v2, /device:TPU:0, one launch (start us, length us, event | category | flops | bytes accessed | tf_op | source)
XLA Modules:
  0.0 55.7 jit_solution(922963919725412562)
XLA Ops:
  0.6 0.0 copy-start.1
  1.3 0.0 copy-start
  1.3 0.7 %broadcast_in_dim.6.id_ref = s32[1,729]{1,0:T(1,128)S(1)} reshape(s32[729]{0:T(1024)} %param.9) | data formatting | bytes 5832 | tf_op jit(solution)/shard_map/broadcast_in_dim | solution.py:378
  2.0 0.7 %broadcast_in_dim.7.ok_ref = s32[1,729]{1,0:T(1,128)S(1)} reshape(s32[729]{0:T(1024)} %param.10) | data formatting | bytes 5832 | tf_op jit(solution)/shard_map/broadcast_in_dim | solution.py:378
  2.7 0.0 copy-done.1
  2.7 0.0 copy-done
  2.7 0.0 copy-start.2
  2.7 0.7 %copy-done.2 = f32[729,3]{0,1:T(4,128)S(1)} copy-done((f32[729,3]{0,1:T(4,128)S(1)}, f32[729,3]{0,1:T(4,128)}, u32[]{:S(2)}) %copy-start.2) | copy-done | bytes 8772
  3.4 18.3 %exchange.1 = (f32[16,768]{1,0:T(8,128)S(1)}, f32[17,4,768]{2,1,0:T(4,128)S(1)}) custom-call(f32[3,729]{1,0:T(4,128)S(1)} %bitcast.12, f32[3,729]{1,0:T(4,128)S(1)} %bitcast.13, f32[3,729]{1,0:T(4,128)S(1)} %bitcast.14, s32[1,729]{1,0:T(1,128)S(1)} %broadcast_in_dim.6.id_ref, s32[1,729]{1,0:T(1,128)S(1)} %broadcast_in_dim.7.ok_ref, f32[1,1]{1,0:T(1,128)} %bitcast.10.side_ref), custom_call_target="tpu_custom_call" | custom-call | tf_op jit(solution)/shard_map/exchange/pallas_call | solution.py:366
  21.8 20.8 %forces.1 = (f32[3,729]{1,0:T(4,128)}, f32[3,729]{1,0:T(4,128)}, f32[3,729]{1,0:T(4,128)}, s32[1,729]{1,0:T(1,128)S(1)}, s32[1,729]{1,0:T(1,128)S(1)}, /*index=5*/f32[1,128]{1,0:T(1,128)S(1)}) custom-call(f32[16,768]{1,0:T(8,128)S(1)} %get-tuple-element.14.srt_ref, f32[17,4,768]{2,1,0:T(4,128)S(1)} %get-tuple-element.15.gh_ref, s32[17,32]{1,0:T(8,128)S(1)} %fusion.offs_ref, ...), custom_call_target="tpu_custom_call" | custom-call | tf_op jit(solution)/shard_map/forces/pallas_call | solution.py:382
  42.5 0.0 copy-start.3
  42.5 0.5 copy-done.3
  43.0 9.8 %total.1 = f32[1,1]{1,0:T(1,128)} custom-call(f32[1,128]{1,0:T(1,128)} %copy-done.3), custom_call_target="tpu_custom_call" | custom-call | tf_op jit(solution)/shard_map/total/pallas_call | solution.py:391
  52.8 0.6 %reduce = s32[729]{0:T(1024)} reduce(s32[1,729]{1,0:T(1,128)S(1)} %get-tuple-element.19, s32[]{:T(128)} %constant.5), dimensions={0}, to_apply=%get-tuple-element.19.reduce_sub_computation | reduce | bytes 5836 | tf_op jit(solution)/shard_map/forces/pallas_call | solution.py:382
  53.4 0.6 %reduce.1 = s32[729]{0:T(1024)} reduce(s32[1,729]{1,0:T(1,128)S(1)} %get-tuple-element.20, s32[]{:T(128)} %constant.5), dimensions={0}, to_apply=%get-tuple-element.20.reduce_sub_computation | reduce | bytes 5836 | tf_op jit(solution)/shard_map/forces/pallas_call | solution.py:382
  (2 shorter events, 0.1 us)
Async XLA Ops:
  0.6 2.1 %copy-start.1 = (f32[729,3]{0,1:T(4,128)S(1)}, f32[729,3]{0,1:T(4,128)}, u32[]{:S(2)}) copy-start(f32[729,3]{0,1:T(4,128)} %param.7) | copy-start | bytes 26248
  1.3 1.4 %copy-start = (f32[729,3]{0,1:T(4,128)S(1)}, f32[729,3]{0,1:T(4,128)}, u32[]{:S(2)}) copy-start(f32[729,3]{0,1:T(4,128)} %param.6) | copy-start | bytes 26248
  2.7 0.7 %copy-start.2 = (f32[729,3]{0,1:T(4,128)S(1)}, f32[729,3]{0,1:T(4,128)}, u32[]{:S(2)}) copy-start(f32[729,3]{0,1:T(4,128)} %param.8) | copy-start | bytes 26248
  42.5 0.5 copy-start.3

commit v3 on v2

--- a/solution.py
+++ b/solution.py
@@ -16,6 +16,8 @@
 DIRS = [(dx, dy, dz) for dz in (-1, 0, 1) for dy in (-1, 0, 1) for dx in (-1, 0, 1) if (dx, dy, dz) != (0, 0, 0)]
 NEAR = RC + 1.0e-3
 PACK = 8
+CHUNK = 4
+GROUPS = 4
 L = 128
 F32 = jnp.float32
 BF16 = jnp.bfloat16
@@ -222,41 +224,36 @@
         copy.wait_send()
 
 
-def force_kernel(sizes, peers, slots, unroll, srt_ref, gh_ref, offs_ref, side_ref, pos_ref, vel_ref, frc_ref, id_ref, ok_ref, en_ref, rolled, cols, acc):
+def force_kernel(sizes, peers, slots, srt_ref, gh_ref, offs_ref, side_ref, pos_ref, vel_ref, frc_ref, id_ref, ok_ref, en_ref, line, wide_line, own_cols, sums):
     size_x, size_y, size_z = sizes
     me = (lax.axis_index("x"), lax.axis_index("y"), lax.axis_index("z"))
     n = pos_ref.shape[1]
     side = side_ref[0, 0]
-    tiles = slots // L
     okrow = srt_ref[8:9]
-    own = jnp.where(okrow > 0.5, srt_ref[0:3], -FAR)
+    good = okrow > 0.5
     count = jnp.sum(okrow).astype(I32)
-    wide = side > 2.0 * NEAR
-
-    def put(block, length, start):
-        rolled[...] = block
-
-        def one(t, carry):
-            tile = rolled[:, pl.ds(pl.multiple_of(t * L, L), L)]
-            cols[pl.ds(pl.multiple_of(start + t * L, 8), L), 0:8] = jnp.transpose(tile)
-            return carry
-
-        lax.fori_loop(0, (length + 127) // L, one, 0)
-        return start + ((length + 7) // 8) * 8
+    spread = side > 2.0 * NEAR
+    span = slots + L
+
+    parts = [part.astype(F32) for part in split3(jnp.where(good, srt_ref[0:3], -FAR))]
+    parts = jnp.concatenate(parts + [jnp.zeros((7, slots), F32)], axis=0)
+    row = lax.broadcasted_iota(I32, (16, 3 * L), 0)
+    tile = lax.broadcasted_iota(I32, (16, 3 * L), 1) // L
+    picks = jnp.where((row == tile) | (row == tile + 3) | (row == tile + 6), 1.0, 0.0).astype(BF16)
+    own_cols[...] = lax.dot_general(jnp.transpose(parts).astype(BF16), picks, NN, preferred_element_type=F32)
 
     pad5 = jnp.zeros((5, slots), F32)
-    fill = put(jnp.concatenate([jnp.where(okrow > 0.5, srt_ref[0:3], FAR), pad5], axis=0), count, jnp.int32(0))
-    spare = jnp.full((8 * unroll, 8), FAR, F32)
-    cols[pl.ds(pl.multiple_of(fill, 8), 8 * unroll), 0:8] = spare
-    self_steps = (fill // 8 + unroll - 1) // unroll
-    fill = self_steps * (8 * unroll)
+    away = jnp.full((8, L), FAR, F32)
+    line[:, 0:span] = jnp.concatenate([jnp.concatenate([jnp.where(good, srt_ref[0:3], FAR), pad5], axis=0), away], axis=1)
+    lane = lax.broadcasted_iota(I32, (8, span), 1)
+    fill = count
     for d in DIRS:
         offset = (d[0] % size_x, d[1] % size_y, d[2] % size_z)
         back = ((-offset[0]) % size_x, (-offset[1]) % size_y, (-offset[2]) % size_z)
         index = peers.index(back)
         first, last = range_of(d)
-        begin = jnp.where(wide, offs_ref[index, first], 0)
-        end = jnp.where(wide, offs_ref[index, last], offs_ref[index, 27])
+        begin = jnp.where(spread, offs_ref[index, first], 0)
+        end = jnp.where(spread, offs_ref[index, last], offs_ref[index, 27])
         shifts = []
         for axis in range(3):
             box = side * float(sizes[axis])
@@ -267,23 +264,42 @@
             else:
                 shifts.append(jnp.float32(0.0))
         block = jnp.concatenate([gh_ref[index, a:a + 1] + shifts[a] for a in range(3)] + [pad5], axis=0)
-        block = pltpu.roll(block, lax.rem(slots - begin, slots), 1)
-        fill = put(block, end - begin, fill)
-    cols[pl.ds(pl.multiple_of(fill, 8), 8 * unroll), 0:8] = spare
-    steps = (fill // 8 + unroll - 1) // unroll
-
-    def sweep(used):
-        ox, oy, oz = [[jnp.broadcast_to(own[a:a + 1, t * L:t * L + L], (8, L)) for t in range(used)] for a in range(3)]
-
-        def body(with_self, i, carry):
-            fx, fy, fz, en = list(carry[0]), list(carry[1]), list(carry[2]), carry[3]
-            for u in range(unroll):
-                col = cols[pl.ds(pl.multiple_of((i * unroll + u) * 8, 8), 8), :]
-                gx, gy, gz = [jnp.broadcast_to(col[:, a:a + 1], (8, L)) for a in range(3)]
-                for t in range(used):
-                    dx = ox[t] - gx
-                    dy = oy[t] - gy
-                    dz = oz[t] - gz
+        block = jnp.concatenate([block, away], axis=1)
+        head = fill & (L - 1)
+        base = pl.multiple_of(fill - head, L)
+        move = head - begin
+        block = pltpu.roll(block, jnp.where(move < 0, move + span, move), 1)
+        tail = head + end - begin
+        block = jnp.where(lane < tail, block, FAR)
+        line[:, pl.ds(base, L)] = jnp.where(lane[:, 0:L] < head, line[:, pl.ds(base, L)], block[:, 0:L])
+        line[:, pl.ds(pl.multiple_of(base + L, L), slots)] = block[:, L:]
+        fill = fill + (end - begin)
+    rest = pl.multiple_of(((fill + L - 1) // L) * L, L)
+    line[:, pl.ds(rest, CHUNK * L)] = jnp.full((8, CHUNK * L), FAR, F32)
+    self_chunks = (count + CHUNK * L - 1) // (CHUNK * L)
+    chunks = (fill + CHUNK * L - 1) // (CHUNK * L)
+
+    def widen(c, carry):
+        for t in range(CHUNK):
+            place = pl.ds(pl.multiple_of((c * CHUNK + t) * L, L), L)
+            tile = line[:, place]
+            for a in range(3):
+                wide_line[a, :, place] = jnp.broadcast_to(tile[a:a + 1], (8, L))
+        return carry
+
+    lax.fori_loop(0, chunks, widen, 0)
+
+    def own_step(q, energy):
+        rows = [pl.ds(pl.multiple_of((q * GROUPS + g) * 8, 8), 8) for g in range(GROUPS)]
+        own = [[own_cols[rows[g], a * L:a * L + L] for a in range(3)] for g in range(GROUPS)]
+
+        def body(with_self, c, carry):
+            force, en = [list(f) for f in carry[0]], carry[1]
+            for t in range(CHUNK):
+                place = pl.ds(pl.multiple_of((c * CHUNK + t) * L, L), L)
+                near_xyz = [wide_line[a, :, place] for a in range(3)]
+                for g in range(GROUPS):
+                    dx, dy, dz = [own[g][a] - near_xyz[a] for a in range(3)]
                     d2 = dx * dx + dy * dy + dz * dz
                     near = d2 < RC * RC
                     if with_self:
@@ -296,29 +312,32 @@
                     w = inv * (UPC / 24.0)
                     scale = (p + s12) * s2 + w
                     en = en + ((p + jnp.where(near, 0.25 * (RC * UPC - UCUT), 0.0)) - 6.0 * (w * d2))
-                    fx[t] = fx[t] + scale * dx
-                    fy[t] = fy[t] + scale * dy
-                    fz[t] = fz[t] + scale * dz
-            return tuple(fx), tuple(fy), tuple(fz), en
+                    force[g] = [force[g][0] + scale * dx, force[g][1] + scale * dy, force[g][2] + scale * dz]
+            return tuple(tuple(f) for f in force), en
 
         zero = jnp.zeros((8, L), F32)
-        sums = lax.fori_loop(0, self_steps, functools.partial(body, True), ((zero,) * used,) * 3 + (zero,))
-        sums = lax.fori_loop(self_steps, steps, functools.partial(body, False), sums)
-        for a in range(3):
-            for t in range(used):
-                acc[a:a + 1, t * L:t * L + L] = 24.0 * jnp.sum(sums[a][t], axis=0, keepdims=True)
-        en_ref[...] = 2.0 * jnp.sum(sums[3], axis=0, keepdims=True)
-
-    acc[...] = jnp.zeros_like(acc)
-    need = (count + L - 1) // L
-    pl.when(need <= 3)(functools.partial(sweep, min(3, tiles)))
-    for used in range(4, tiles + 1):
-        pl.when(need == used)(functools.partial(sweep, used))
-
-    force = acc[0:3] * okrow
+        carry = (((zero,) * 3,) * GROUPS, energy)
+        carry = lax.fori_loop(0, self_chunks, functools.partial(body, True), carry)
+        force, energy = lax.fori_loop(self_chunks, chunks, functools.partial(body, False), carry)
+        for g in range(GROUPS):
+            for a in range(3):
+                sums[a, rows[g], :] = force[g][a]
+        return energy
+
+    own_steps = (count + 8 * GROUPS - 1) // (8 * GROUPS)
+    energy = lax.fori_loop(0, own_steps, own_step, jnp.zeros((8, L), F32))
+    en_ref[...] = 2.0 * jnp.sum(energy, axis=0, keepdims=True)
+
+    col = lax.broadcasted_iota(I32, (L, L), 1)
+    total = jnp.zeros((slots, L), F32)
+    for a in range(3):
+        pick = jnp.where(col == a, 1.0, 0.0).astype(BF16)
+        for part in split3(sums[a]):
+            total = total + lax.dot_general(part, pick, NN, preferred_element_type=F32)
+    force = jnp.where(good, 24.0 * jnp.transpose(total)[0:3], 0.0)
     pos_ref[...] = srt_ref[0:3, 0:n]
     frc_ref[...] = force[:, 0:n]
-    vel_ref[...] = ((srt_ref[3:6] + (0.5 * DT) * force) * okrow)[:, 0:n]
+    vel_ref[...] = (srt_ref[3:6] + (0.5 * DT) * force)[:, 0:n]
     id_ref[...] = (srt_ref[6:7].astype(I32) * 65536 + srt_ref[7:8].astype(I32))[:, 0:n]
     ok_ref[...] = okrow[:, 0:n].astype(I32)
 
@@ -355,7 +374,6 @@
     sizes = (mesh.shape["x"], mesh.shape["y"], mesh.shape["z"])
     peers = sorted({(d[0] % sizes[0], d[1] % sizes[1], d[2] % sizes[2]) for d in DIRS} - {(0, 0, 0)})
     devices = sizes[0] * sizes[1] * sizes[2]
-    unroll = 2
 
     def local_step(atom_pos, atom_vel, atom_frc, atom_id, atom_ok, brick_side):
         n = atom_pos.shape[0]
@@ -380,11 +398,11 @@
         out_f = jax.ShapeDtypeStruct((3, n), F32)
         out_i = jax.ShapeDtypeStruct((1, n), I32)
         new_pos, new_vel, new_frc, new_id, new_ok, energy = pl.pallas_call(
-            functools.partial(force_kernel, sizes, peers, slots, unroll),
+            functools.partial(force_kernel, sizes, peers, slots),
             out_shape=(out_f, out_f, out_f, out_i, out_i, jax.ShapeDtypeStruct((1, L), F32)),
             in_specs=[vmem, vmem, smem, smem],
             out_specs=(vmem,) * 6,
-            scratch_shapes=[pltpu.VMEM((8, slots), F32), pltpu.VMEM((27 * slots + L + 8 * unroll, L), F32), pltpu.VMEM((3, slots), F32)],
+            scratch_shapes=[pltpu.VMEM((8, 28 * slots + CHUNK * L), F32), pltpu.VMEM((3, 8, 28 * slots + CHUNK * L), F32), pltpu.VMEM((slots, 3 * L), F32), pltpu.VMEM((3, slots, L), F32)],
             compiler_params=pltpu.CompilerParams(vmem_limit_bytes=40 * 2 ** 20),
             name="forces",
         )(srt, ghosts, offs, side)

time: 55.7 us -> 42.8 us (0.77)
  Pallas kernels: 48.8 us -> 35.8 us
    pallas_call x1, Pallas kernels: 20.8 us -> 7.38 us  [local_step(): pl.pallas_call(functools.partial(force_kernel, sizes, peers, slots), out_...]
where the time goes in v3:
time: 42.8 us; the launch traced here: 42.7 us
  Pallas kernels  35.8 us (84%)
  between operations  3.04 us (7%)
  local copies, waits for them, and re-layouts  2.65 us (6%)
  other arithmetic  1.22 us (3%)
    pallas_call x1, Pallas kernels, local_step(): pl.pallas_call(functools.partial(exchange_kernel, sizes, peers, slots), o...  18.3 us
    pallas_call x1, Pallas kernels, local_step(): pl.pallas_call(functools.partial(total_kernel, sizes), out_shape=jax.Shap...  10.1 us
    pallas_call x1, Pallas kernels, local_step(): pl.pallas_call(functools.partial(force_kernel, sizes, peers, slots), out_...  7.38 us
    unnamed x8, local copies, waits for them, and re-layouts  1.22 us
    pallas_call x2, other arithmetic, local_step(): pl.pallas_call(functools.partial(force_kernel, sizes, peers, slots), out_...  1.21 us

profile of v3, /device:TPU:0, one launch (start us, length us, event | category | flops | bytes accessed | tf_op | source)
XLA Modules:
  0.0 42.7 jit_solution(12043462722564046862)
XLA Ops:
  0.6 0.0 copy-start.1
  1.3 0.0 copy-start
  1.3 0.7 %broadcast_in_dim.6.id_ref = s32[1,729]{1,0:T(1,128)S(1)} reshape(s32[729]{0:T(1024)} %param.9) | data formatting | bytes 5832 | tf_op jit(solution)/shard_map/broadcast_in_dim | solution.py:396
  2.0 0.7 %broadcast_in_dim.7.ok_ref = s32[1,729]{1,0:T(1,128)S(1)} reshape(s32[729]{0:T(1024)} %param.10) | data formatting | bytes 5832 | tf_op jit(solution)/shard_map/broadcast_in_dim | solution.py:396
  2.7 0.0 copy-done.1
  2.7 0.0 copy-done
  2.7 0.0 copy-start.2
  2.7 0.7 %copy-done.2 = f32[729,3]{0,1:T(4,128)S(1)} copy-done((f32[729,3]{0,1:T(4,128)S(1)}, f32[729,3]{0,1:T(4,128)}, u32[]{:S(2)}) %copy-start.2) | copy-done | bytes 8772
  3.4 18.3 %exchange.1 = (f32[16,768]{1,0:T(8,128)S(1)}, f32[17,4,768]{2,1,0:T(4,128)S(1)}) custom-call(f32[3,729]{1,0:T(4,128)S(1)} %bitcast.12, f32[3,729]{1,0:T(4,128)S(1)} %bitcast.13, f32[3,729]{1,0:T(4,128)S(1)} %bitcast.14, s32[1,729]{1,0:T(1,128)S(1)} %broadcast_in_dim.6.id_ref, s32[1,729]{1,0:T(1,128)S(1)} %broadcast_in_dim.7.ok_ref, f32[1,1]{1,0:T(1,128)} %bitcast.10.side_ref), custom_call_target="tpu_custom_call" | custom-call | tf_op jit(solution)/shard_map/exchange/pallas_call | solution.py:384
  21.8 7.4 %forces.1 = (f32[3,729]{1,0:T(4,128)}, f32[3,729]{1,0:T(4,128)}, f32[3,729]{1,0:T(4,128)}, s32[1,729]{1,0:T(1,128)S(1)}, s32[1,729]{1,0:T(1,128)S(1)}, /*index=5*/f32[1,128]{1,0:T(1,128)S(1)}) custom-call(f32[16,768]{1,0:T(8,128)S(1)} %get-tuple-element.14.srt_ref, f32[17,4,768]{2,1,0:T(4,128)S(1)} %get-tuple-element.15.gh_ref, s32[17,32]{1,0:T(8,128)S(1)} %fusion.offs_ref, ...), custom_call_target="tpu_custom_call" | custom-call | tf_op jit(solution)/shard_map/forces/pallas_call | solution.py:400
  29.1 0.0 copy-start.3
  29.1 0.5 %copy-done.3 = f32[1,128]{1,0:T(1,128)} copy-done((f32[1,128]{1,0:T(1,128)}, f32[1,128]{1,0:T(1,128)S(1)}, u32[]{:S(2)}) %copy-start.3) | copy-done | bytes 536
  29.6 10.1 %total.1 = f32[1,1]{1,0:T(1,128)} custom-call(f32[1,128]{1,0:T(1,128)} %copy-done.3), custom_call_target="tpu_custom_call" | custom-call | tf_op jit(solution)/shard_map/total/pallas_call | solution.py:409
  39.8 0.6 %reduce = s32[729]{0:T(1024)} reduce(s32[1,729]{1,0:T(1,128)S(1)} %get-tuple-element.19, s32[]{:T(128)} %constant.5), dimensions={0}, to_apply=%get-tuple-element.19.reduce_sub_computation | reduce | bytes 5836 | tf_op jit(solution)/shard_map/forces/pallas_call | solution.py:400
  40.4 0.6 %reduce.1 = s32[729]{0:T(1024)} reduce(s32[1,729]{1,0:T(1,128)S(1)} %get-tuple-element.20, s32[]{:T(128)} %constant.5), dimensions={0}, to_apply=%get-tuple-element.20.reduce_sub_computation | reduce | bytes 5836 | tf_op jit(solution)/shard_map/forces/pallas_call | solution.py:400
  (2 shorter events, 0.1 us)
Async XLA Ops:
  0.6 2.1 %copy-start.1 = (f32[729,3]{0,1:T(4,128)S(1)}, f32[729,3]{0,1:T(4,128)}, u32[]{:S(2)}) copy-start(f32[729,3]{0,1:T(4,128)} %param.7) | copy-start | bytes 26248
  1.3 1.4 %copy-start = (f32[729,3]{0,1:T(4,128)S(1)}, f32[729,3]{0,1:T(4,128)}, u32[]{:S(2)}) copy-start(f32[729,3]{0,1:T(4,128)} %param.6) | copy-start | bytes 26248
  2.7 0.7 %copy-start.2 = (f32[729,3]{0,1:T(4,128)S(1)}, f32[729,3]{0,1:T(4,128)}, u32[]{:S(2)}) copy-start(f32[729,3]{0,1:T(4,128)} %param.8) | copy-start | bytes 26248
  29.1 0.5 %copy-start.3 = (f32[1,128]{1,0:T(1,128)}, f32[1,128]{1,0:T(1,128)S(1)}, u32[]{:S(2)}) copy-start(f32[1,128]{1,0:T(1,128)S(1)} %get-tuple-element.21.part_ref) | copy-start | bytes 1540

commit v4 on v3

--- a/solution.py
+++ b/solution.py
@@ -110,25 +110,32 @@
     return jnp.concatenate([x, jnp.zeros((x.shape[0], width - x.shape[1]), x.dtype)], axis=1)
 
 
-def exchange_kernel(sizes, peers, slots, pos_ref, vel_ref, frc_ref, id_ref, ok_ref, side_ref, srt_ref, gh_ref, pkt, rcv, out3, psend, precv, gsend, grecv):
+def exchange_kernel(sizes, peers, slots, pos_hbm, vel_hbm, frc_hbm, id_hbm, ok_hbm, side_ref, srt_ref, gh_ref, pos_ref, vel_ref, frc_ref, id_ref, ok_ref, pkt, rcv, out3, isem, psend, precv, gsend, grecv):
     size_x, size_y, size_z = sizes
     me = (lax.axis_index("x"), lax.axis_index("y"), lax.axis_index("z"))
 
     def device_at(offset):
         return (lax.rem(me[2] + offset[2], size_z), lax.rem(me[1] + offset[1], size_y), lax.rem(me[0] + offset[0], size_x))
 
+    loads = []
+    for index, (src, dst) in enumerate(((ok_hbm, ok_ref), (id_hbm, id_ref), (pos_hbm, pos_ref), (vel_hbm, vel_ref), (frc_hbm, frc_ref))):
+        load = pltpu.make_async_copy(src, dst, isem.at[index])
+        load.start()
+        loads.append(load)
     barrier = pltpu.get_barrier_semaphore()
     for offset in peers:
         pl.semaphore_signal(barrier, inc=1, device_id=device_at(offset), device_id_type=pl.DeviceIdType.MESH)
 
     n = pos_ref.shape[1]
     side = side_ref[0, 0]
-    owned = pad_lanes(ok_ref[...], slots) > 0
+    for load in loads:
+        load.wait()
+    owned = pad_lanes(jnp.reshape(ok_ref[...], (1, n)), slots) > 0
     half = vel_ref[...] + (0.5 * DT) * frc_ref[...]
     free = pos_ref[...] + DT * half
     half = pad_lanes(half, slots)
     free = pad_lanes(free, slots)
-    ids = pad_lanes(id_ref[...], slots)
+    ids = pad_lanes(jnp.reshape(id_ref[...], (1, n)), slots)
     code = jnp.zeros((1, slots), I32)
     moved = []
     low_side = []
@@ -338,8 +345,8 @@
     pos_ref[...] = srt_ref[0:3, 0:n]
     frc_ref[...] = force[:, 0:n]
     vel_ref[...] = (srt_ref[3:6] + (0.5 * DT) * force)[:, 0:n]
-    id_ref[...] = (srt_ref[6:7].astype(I32) * 65536 + srt_ref[7:8].astype(I32))[:, 0:n]
-    ok_ref[...] = okrow[:, 0:n].astype(I32)
+    id_ref[...] = jnp.reshape((srt_ref[6:7].astype(I32) * 65536 + srt_ref[7:8].astype(I32))[:, 0:n], (n,))
+    ok_ref[...] = jnp.reshape(okrow[:, 0:n].astype(I32), (n,))
 
 
 def total_kernel(sizes, part_ref, sum_ref, rows, ssem, rsem):
@@ -384,19 +391,20 @@
         srt, ghosts = pl.pallas_call(
             functools.partial(exchange_kernel, sizes, peers, slots),
             out_shape=(jax.ShapeDtypeStruct((16, slots), F32), jax.ShapeDtypeStruct((len(peers), 4, slots), F32)),
-            in_specs=[vmem] * 5 + [smem],
+            in_specs=[pl.BlockSpec(memory_space=pltpu.HBM)] * 5 + [smem],
             out_specs=(vmem, vmem),
             scratch_shapes=[
+                pltpu.VMEM((3, n), F32), pltpu.VMEM((3, n), F32), pltpu.VMEM((3, n), F32), pltpu.VMEM((n,), I32), pltpu.VMEM((n,), I32),
                 pltpu.VMEM((26 * PACK, L), F32), pltpu.VMEM((26 * PACK, L), F32), pltpu.VMEM((3, 4, slots), F32),
-                pltpu.SemaphoreType.DMA((26,)), pltpu.SemaphoreType.DMA((26,)),
+                pltpu.SemaphoreType.DMA((5,)), pltpu.SemaphoreType.DMA((26,)), pltpu.SemaphoreType.DMA((26,)),
                 pltpu.SemaphoreType.DMA((len(peers),)), pltpu.SemaphoreType.DMA((len(peers),)),
             ],
             compiler_params=pltpu.CompilerParams(collective_id=0, has_side_effects=True, vmem_limit_bytes=40 * 2 ** 20),
             name="exchange",
-        )(atom_pos.T, atom_vel.T, atom_frc.T, atom_id[None, :], atom_ok[None, :], side)
+        )(*[pltpu.with_memory_space_constraint(v, pltpu.HBM) for v in (atom_pos.T, atom_vel.T, atom_frc.T, atom_id, atom_ok)], side)
         offs = ghosts[:, 3, 0:32].astype(I32)
         out_f = jax.ShapeDtypeStruct((3, n), F32)
-        out_i = jax.ShapeDtypeStruct((1, n), I32)
+        out_i = jax.ShapeDtypeStruct((n,), I32)
         new_pos, new_vel, new_frc, new_id, new_ok, energy = pl.pallas_call(
             functools.partial(force_kernel, sizes, peers, slots),
             out_shape=(out_f, out_f, out_f, out_i, out_i, jax.ShapeDtypeStruct((1, L), F32)),
@@ -414,8 +422,8 @@
             scratch_shapes=[pltpu.VMEM((devices, L), F32), pltpu.SemaphoreType.DMA((devices,)), pltpu.SemaphoreType.DMA((devices,))],
             compiler_params=pltpu.CompilerParams(collective_id=1, has_side_effects=True),
             name="total",
-        )(energy)[0, 0]
-        return new_pos.T, new_vel.T, new_frc.T, new_id[0], new_ok[0], energy
+        )(pltpu.with_memory_space_constraint(energy, pltpu.VMEM))[0, 0]
+        return new_pos.T, new_vel.T, new_frc.T, new_id, new_ok, energy
 
     row_spec = P(MESH_AXES, None)
     id_spec = P(MESH_AXES)

time: 42.8 us -> 38.2 us (0.89)
  local copies, waits for them, and re-layouts: 2.65 us -> 0.05 us
  other arithmetic: 1.22 us -> 0.01 us
  Pallas kernels: 35.8 us -> 34.7 us
    pallas_call x1, Pallas kernels: 10.1 us -> 8.64 us  [local_step(): pl.pallas_call(functools.partial(total_kernel, sizes), out_shape=jax.Shap...]
    broadcast_in_dim x2 -> x0, local copies, waits for them, and re-layouts: 1.38 us -> none  [the longest x1 0.7 us: local_step(): atom_id[None, :]]
    unnamed x8 -> x0, local copies, waits for them, and re-layouts: 1.22 us -> none
    pallas_call x2 -> x0, other arithmetic: 1.21 us -> none  [local_step(): pl.pallas_call(functools.partial(force_kernel, sizes, peers, slots), out_...]
where the time goes in v4:
time: 38.2 us; the launch traced here: 37.9 us
  Pallas kernels  34.7 us (91%)
  between operations  3.07 us (8%)
    pallas_call x1, Pallas kernels, local_step(): pl.pallas_call(functools.partial(exchange_kernel, sizes, peers, slots), o...  18.4 us
    pallas_call x1, Pallas kernels, local_step(): pl.pallas_call(functools.partial(total_kernel, sizes), out_shape=jax.Shap...  8.64 us
    pallas_call x1, Pallas kernels, local_step(): pl.pallas_call(functools.partial(force_kernel, sizes, peers, slots), out_...  7.72 us

profile of v4, /device:TPU:0, one launch (start us, length us, event | category | flops | bytes accessed | tf_op | source)
XLA Modules:
  0.0 37.9 jit_solution(17888628600237828461)
XLA Ops:
  1.3 18.4 %exchange.1 = (f32[16,768]{1,0:T(8,128)S(1)}, f32[17,4,768]{2,1,0:T(4,128)S(1)}) custom-call(f32[3,729]{1,0:T(4,128)} %bitcast.12, f32[3,729]{1,0:T(4,128)} %bitcast.13, f32[3,729]{1,0:T(4,128)} %bitcast.14, s32[729]{0:T(1024)} %id_hbm.1, s32[729]{0:T(1024)} %ok_hbm.1, f32[1,1]{1,0:T(1,128)} %bitcast.10.side_ref), custom_call_target="tpu_custom_call" | custom-call | tf_op jit(solution)/shard_map/exchange/pallas_call | solution.py:391
  19.7 7.7 %forces.1 = (f32[3,729]{1,0:T(4,128)}, f32[3,729]{1,0:T(4,128)}, f32[3,729]{1,0:T(4,128)}, s32[729]{0:T(1024)}, s32[729]{0:T(1024)}, /*index=5*/f32[1,128]{1,0:T(1,128)S(1)}) custom-call(f32[16,768]{1,0:T(8,128)S(1)} %get-tuple-element.14.srt_ref, f32[17,4,768]{2,1,0:T(4,128)S(1)} %get-tuple-element.15.gh_ref, s32[17,32]{1,0:T(8,128)S(1)} %fusion.offs_ref, ...), custom_call_target="tpu_custom_call" | custom-call | tf_op jit(solution)/shard_map/forces/pallas_call | solution.py:408
  27.5 8.6 %total.1 = f32[1,1]{1,0:T(1,128)} custom-call(f32[1,128]{1,0:T(1,128)S(1)} %get-tuple-element.21.part_ref), custom_call_target="tpu_custom_call" | custom-call | tf_op jit(solution)/shard_map/total/pallas_call | solution.py:417
  (2 shorter events, 0.1 us)

commit v5 on v4

--- a/solution.py
+++ b/solution.py
@@ -16,6 +16,7 @@
 DIRS = [(dx, dy, dz) for dz in (-1, 0, 1) for dy in (-1, 0, 1) for dx in (-1, 0, 1) if (dx, dy, dz) != (0, 0, 0)]
 NEAR = RC + 1.0e-3
 PACK = 8
+NEW = 256
 CHUNK = 4
 GROUPS = 4
 L = 128
@@ -110,7 +111,7 @@
     return jnp.concatenate([x, jnp.zeros((x.shape[0], width - x.shape[1]), x.dtype)], axis=1)
 
 
-def exchange_kernel(sizes, peers, slots, pos_hbm, vel_hbm, frc_hbm, id_hbm, ok_hbm, side_ref, srt_ref, gh_ref, pos_ref, vel_ref, frc_ref, id_ref, ok_ref, pkt, rcv, out3, isem, psend, precv, gsend, grecv):
+def exchange_kernel(sizes, peers, slots, pos_hbm, vel_hbm, frc_hbm, id_hbm, ok_hbm, side_ref, srt_ref, gh_ref, ga_ref, pos_ref, vel_ref, frc_ref, id_ref, ok_ref, pkt, rcv, out3, new3, isem, psend, precv, gsend, grecv, asend, arecv):
     size_x, size_y, size_z = sizes
     me = (lax.axis_index("x"), lax.axis_index("y"), lax.axis_index("z"))
 
@@ -156,62 +157,73 @@
 
     place, _ = class_places(code, False)
     leaving = owned & (code != 13)
-    target = jnp.where(leaving, (code - jnp.where(code > 13, 1, 0)) * PACK + place.astype(I32), -1)
-    hot = onehot_rows(target, 0, 26 * PACK)
-    parts = split3(data)
-    got = lax.dot_general(hot, parts[0], NT, preferred_element_type=F32)
-    got = got + lax.dot_general(hot, parts[1], NT, preferred_element_type=F32)
-    got = got + lax.dot_general(hot, parts[2], NT, preferred_element_type=F32)
-    pkt[...] = jnp.concatenate([got, jnp.zeros((26 * PACK, 112), F32)], axis=1)
-
-    pl.semaphore_wait(barrier, len(peers))
-    copies = []
-    for index, d in enumerate(DIRS):
-        offset = (d[0] % size_x, d[1] % size_y, d[2] % size_z)
+    way = jnp.where(leaving, code - jnp.where(code > 13, 1, 0), 31)
+    member = jnp.where(lax.broadcasted_iota(I32, (32, slots), 0) == way, 1.0, 0.0).astype(BF16)
+    fields = jnp.concatenate([jnp.where(place == float(k), data, 0.0) for k in range(PACK)], axis=0)
+    packed = jnp.zeros((32, L), F32)
+    for part in split3(fields):
+        packed = packed + lax.dot_general(member, part, NT, preferred_element_type=F32)
+    pkt[...] = packed
+
+    def bins_of(pos):
+        bins = []
+        for axis in range(3):
+            loc = pos[axis:axis + 1] - low_side[axis]
+            bins.append(jnp.where(loc < NEAR, 0, jnp.where(loc > side - NEAR, 2, 1)))
+        cx, cy, cz = bins
+        return cz * 9 + cy * 3 + cx, cy * 9 + cx * 3 + cz, cx * 9 + cz * 3 + cy
+
+    eye = lax.broadcasted_iota(I32, (32, L), 0) == lax.broadcasted_iota(I32, (32, L), 1)
+
+    def sorted_block(cand, keys, kept):
+        width = cand.shape[1]
+        where_to, before = class_places(jnp.where(kept, keys, 28), True)
+        arranged = scatter_lanes(cand, jnp.where(kept, where_to.astype(I32), -1), width)
+        total = jnp.concatenate([before[27:28]] * (width // L), axis=1)
+        lane = lax.broadcasted_iota(I32, (1, width), 1).astype(F32)
+        counts = jnp.sum(jnp.where(eye, before, 0.0), axis=0, keepdims=True)
+        return jnp.concatenate([jnp.where(lane < total, arranged[0:3], FAR), pad_lanes(counts, width)], axis=0)
+
+    sent = []
+
+    def send(src, dst, ssem, rsem, offset):
         copy = pltpu.make_async_remote_copy(
-            src_ref=pkt.at[pl.ds(index * PACK, PACK)], dst_ref=rcv.at[pl.ds(index * PACK, PACK)],
-            send_sem=psend.at[index], recv_sem=precv.at[index],
+            src_ref=src, dst_ref=dst, send_sem=ssem, recv_sem=rsem,
             device_id=device_at(offset), device_id_type=pl.DeviceIdType.MESH)
         copy.start()
-        copies.append(copy)
+        sent.append(copy)
+        return copy
+
+    def send_blocks(block, dst, ssem, rsem, kind):
+        out = []
+        for index, offset in enumerate(peers):
+            if order_of(tuple(0 if c == 0 else 1 for c in offset)) == kind:
+                out.append(send(block.at[kind], dst.at[index], ssem.at[index], rsem.at[index], offset))
+        return out
+
     staying = code == 13
-    stay_f = jnp.where(staying, 1.0, 0.0)
-    for copy in copies:
+    keys = bins_of(data)
+    for kind in range(2):
+        out3[kind] = sorted_block(data[0:8], keys[kind], staying)
+    pl.semaphore_wait(barrier, len(peers))
+    packets = []
+    for index, d in enumerate(DIRS):
+        row = pl.ds(index, 1)
+        packets.append(send(pkt.at[row], rcv.at[row], psend.at[index], precv.at[index], (d[0] % size_x, d[1] % size_y, d[2] % size_z)))
+    blocks = send_blocks(out3, gh_ref, gsend, grecv, 0) + send_blocks(out3, gh_ref, gsend, grecv, 1)
+    out3[2] = sorted_block(data[0:8], keys[2], staying)
+    blocks = blocks + send_blocks(out3, gh_ref, gsend, grecv, 2)
+    for copy in packets:
         copy.wait_recv()
 
-    came = jnp.concatenate([rcv[...], jnp.zeros((256 - 26 * PACK, L), F32)], axis=0)
+    came = jnp.concatenate([rcv[...], jnp.zeros((32 - 26, L), F32)], axis=0)
+    came = jnp.concatenate([came] + [pltpu.roll(came, L - 16 * k, 1) for k in range(1, PACK)], axis=0)
     came_t = jnp.transpose(came)[0:16]
-    valid = jnp.concatenate([staying, came_t[8:9] > 0.5], axis=1)
-    cand = jnp.concatenate([data, came_t], axis=1)
-    bins = []
-    for axis in range(3):
-        loc = cand[axis:axis + 1] - low_side[axis]
-        bins.append(jnp.where(loc < NEAR, 0, jnp.where(loc > side - NEAR, 2, 1)))
-    cx, cy, cz = bins
-    orders = [cz * 9 + cy * 3 + cx, cy * 9 + cx * 3 + cz, cx * 9 + cz * 3 + cy]
-    lane = lax.broadcasted_iota(I32, (1, slots), 1).astype(F32)
-    eye = lax.broadcasted_iota(I32, (32, L), 0) == lax.broadcasted_iota(I32, (32, L), 1)
-    cand8 = cand[0:8]
-    gcopies = []
+    came_ok = came_t[8:9] > 0.5
+    keys = bins_of(came_t)
     for kind in range(3):
-        key = jnp.where(valid, orders[kind], 28)
-        place, before = class_places(key, True)
-        dest = jnp.where(valid, place.astype(I32), -1)
-        arranged = scatter_lanes(cand8, dest, slots)
-        total = jnp.concatenate([before[27:28]] * (slots // L), axis=1)
-        xyz = jnp.where(lane < total, arranged[0:3], FAR)
-        counts = jnp.sum(jnp.where(eye, before, 0.0), axis=0, keepdims=True)
-        out3[kind] = jnp.concatenate([xyz, pad_lanes(counts, slots)], axis=0)
-        for index, offset in enumerate(peers):
-            sign = tuple(0 if c == 0 else 1 for c in offset)
-            if order_of(sign) != kind:
-                continue
-            copy = pltpu.make_async_remote_copy(
-                src_ref=out3.at[kind], dst_ref=gh_ref.at[index],
-                send_sem=gsend.at[index], recv_sem=grecv.at[index],
-                device_id=device_at(offset), device_id_type=pl.DeviceIdType.MESH)
-            copy.start()
-            gcopies.append(copy)
+        new3[kind] = sorted_block(came_t[0:8], keys[kind], came_ok)
+        blocks = blocks + send_blocks(new3, ga_ref, asend, arecv, kind)
 
     arr_ids = came[:, 6:7].astype(I32) * 65536 + came[:, 7:8].astype(I32)
     arr_ok = came[:, 8:9] > 0.5
@@ -222,16 +234,16 @@
     stay_below = lax.dot_general(jnp.ones((16, slots), BF16), above, NT, preferred_element_type=F32)[0:1]
     stay_place, _ = class_places(jnp.where(staying, 0, 31), False)
     rank = jnp.concatenate([stay_place, stay_below], axis=1) + arrivals_below
-    dest = jnp.where(valid, rank.astype(I32), -1)
-    srt_ref[...] = scatter_lanes(cand, dest, slots)
-
-    for copy in gcopies:
+    dest = jnp.where(jnp.concatenate([staying, came_ok], axis=1), rank.astype(I32), -1)
+    srt_ref[...] = scatter_lanes(jnp.concatenate([data, came_t], axis=1), dest, slots)
+
+    for copy in blocks:
         copy.wait_recv()
-    for copy in copies + gcopies:
+    for copy in sent:
         copy.wait_send()
 
 
-def force_kernel(sizes, peers, slots, srt_ref, gh_ref, offs_ref, side_ref, pos_ref, vel_ref, frc_ref, id_ref, ok_ref, en_ref, line, wide_line, own_cols, sums):
+def force_kernel(sizes, peers, slots, srt_ref, gh_ref, ga_ref, offs_ref, side_ref, pos_ref, vel_ref, frc_ref, id_ref, ok_ref, en_ref, line, wide_line, own_cols, sums):
     size_x, size_y, size_z = sizes
     me = (lax.axis_index("x"), lax.axis_index("y"), lax.axis_index("z"))
     n = pos_ref.shape[1]
@@ -259,8 +271,6 @@
         back = ((-offset[0]) % size_x, (-offset[1]) % size_y, (-offset[2]) % size_z)
         index = peers.index(back)
         first, last = range_of(d)
-        begin = jnp.where(spread, offs_ref[index, first], 0)
-        end = jnp.where(spread, offs_ref[index, last], offs_ref[index, 27])
         shifts = []
         for axis in range(3):
             box = side * float(sizes[axis])
@@ -270,17 +280,20 @@
                 shifts.append(jnp.where(me[axis] == 0, -box, 0.0))
             else:
                 shifts.append(jnp.float32(0.0))
-        block = jnp.concatenate([gh_ref[index, a:a + 1] + shifts[a] for a in range(3)] + [pad5], axis=0)
-        block = jnp.concatenate([block, away], axis=1)
-        head = fill & (L - 1)
-        base = pl.multiple_of(fill - head, L)
-        move = head - begin
-        block = pltpu.roll(block, jnp.where(move < 0, move + span, move), 1)
-        tail = head + end - begin
-        block = jnp.where(lane < tail, block, FAR)
-        line[:, pl.ds(base, L)] = jnp.where(lane[:, 0:L] < head, line[:, pl.ds(base, L)], block[:, 0:L])
-        line[:, pl.ds(pl.multiple_of(base + L, L), slots)] = block[:, L:]
-        fill = fill + (end - begin)
+        for source, entry in ((gh_ref, index), (ga_ref, index + len(peers))):
+            width = source.shape[2]
+            begin = jnp.where(spread, offs_ref[entry, first], 0)
+            end = jnp.where(spread, offs_ref[entry, last], offs_ref[entry, 27])
+            block = jnp.concatenate([source[index, a:a + 1] + shifts[a] for a in range(3)] + [jnp.zeros((5, width), F32)], axis=0)
+            block = jnp.concatenate([block, away], axis=1)
+            head = fill & (L - 1)
+            base = pl.multiple_of(fill - head, L)
+            move = head - begin
+            block = pltpu.roll(block, jnp.where(move < 0, move + (width + L), move), 1)
+            block = jnp.where(lane[:, 0:width + L] < head + end - begin, block, FAR)
+            line[:, pl.ds(base, L)] = jnp.where(lane[:, 0:L] < head, line[:, pl.ds(base, L)], block[:, 0:L])
+            line[:, pl.ds(pl.multiple_of(base + L, L), width)] = block[:, L:]
+            fill = fill + (end - begin)
     rest = pl.multiple_of(((fill + L - 1) // L) * L, L)
     line[:, pl.ds(rest, CHUNK * L)] = jnp.full((8, CHUNK * L), FAR, F32)
     self_chunks = (count + CHUNK * L - 1) // (CHUNK * L)
@@ -388,32 +401,31 @@
         side = jnp.reshape(brick_side, (1, 1))
         vmem = pl.BlockSpec(memory_space=pltpu.VMEM)
         smem = pl.BlockSpec(memory_space=pltpu.SMEM)
-        srt, ghosts = pl.pallas_call(
+        srt, ghosts, fresh = pl.pallas_call(
             functools.partial(exchange_kernel, sizes, peers, slots),
-            out_shape=(jax.ShapeDtypeStruct((16, slots), F32), jax.ShapeDtypeStruct((len(peers), 4, slots), F32)),
+            out_shape=(jax.ShapeDtypeStruct((16, slots), F32), jax.ShapeDtypeStruct((len(peers), 4, slots), F32), jax.ShapeDtypeStruct((len(peers), 4, NEW), F32)),
             in_specs=[pl.BlockSpec(memory_space=pltpu.HBM)] * 5 + [smem],
-            out_specs=(vmem, vmem),
+            out_specs=(vmem,) * 3,
             scratch_shapes=[
                 pltpu.VMEM((3, n), F32), pltpu.VMEM((3, n), F32), pltpu.VMEM((3, n), F32), pltpu.VMEM((n,), I32), pltpu.VMEM((n,), I32),
-                pltpu.VMEM((26 * PACK, L), F32), pltpu.VMEM((26 * PACK, L), F32), pltpu.VMEM((3, 4, slots), F32),
+                pltpu.VMEM((32, L), F32), pltpu.VMEM((26, L), F32), pltpu.VMEM((3, 4, slots), F32), pltpu.VMEM((3, 4, NEW), F32),
                 pltpu.SemaphoreType.DMA((5,)), pltpu.SemaphoreType.DMA((26,)), pltpu.SemaphoreType.DMA((26,)),
-                pltpu.SemaphoreType.DMA((len(peers),)), pltpu.SemaphoreType.DMA((len(peers),)),
-            ],
+            ] + [pltpu.SemaphoreType.DMA((len(peers),))] * 4,
             compiler_params=pltpu.CompilerParams(collective_id=0, has_side_effects=True, vmem_limit_bytes=40 * 2 ** 20),
             name="exchange",
         )(*[pltpu.with_memory_space_constraint(v, pltpu.HBM) for v in (atom_pos.T, atom_vel.T, atom_frc.T, atom_id, atom_ok)], side)
-        offs = ghosts[:, 3, 0:32].astype(I32)
+        offs = jnp.concatenate([ghosts[:, 3, 0:32], fresh[:, 3, 0:32]], axis=0).astype(I32)
         out_f = jax.ShapeDtypeStruct((3, n), F32)
         out_i = jax.ShapeDtypeStruct((n,), I32)
         new_pos, new_vel, new_frc, new_id, new_ok, energy = pl.pallas_call(
             functools.partial(force_kernel, sizes, peers, slots),
             out_shape=(out_f, out_f, out_f, out_i, out_i, jax.ShapeDtypeStruct((1, L), F32)),
-            in_specs=[vmem, vmem, smem, smem],
+            in_specs=[vmem] * 3 + [smem] * 2,
             out_specs=(vmem,) * 6,
             scratch_shapes=[pltpu.VMEM((8, 28 * slots + CHUNK * L), F32), pltpu.VMEM((3, 8, 28 * slots + CHUNK * L), F32), pltpu.VMEM((slots, 3 * L), F32), pltpu.VMEM((3, slots, L), F32)],
             compiler_params=pltpu.CompilerParams(vmem_limit_bytes=40 * 2 ** 20),
             name="forces",
-        )(srt, ghosts, offs, side)
+        )(srt, ghosts, fresh, offs, side)
         energy = pl.pallas_call(
             functools.partial(total_kernel, sizes),
             out_shape=jax.ShapeDtypeStruct((1, 1), F32),

time: 38.2 us -> 37.1 us (0.971)
  Pallas kernels: 34.7 us -> 33.3 us
    pallas_call x1, Pallas kernels: 18.4 us -> 17.2 us  [local_step(): pl.pallas_call(functools.partial(exchange_kernel, sizes, peers, slots), o...]
    pallas_call x1, Pallas kernels: 7.72 us -> 7 us  [local_step(): pl.pallas_call(functools.partial(force_kernel, sizes, peers, slots), out_...]
    pallas_call x1, Pallas kernels: 8.64 us -> 9.18 us  [local_step(): pl.pallas_call(functools.partial(total_kernel, sizes), out_shape=jax.Shap...]
where the time goes in v5:
time: 37.1 us; the launch traced here: 36.5 us
  Pallas kernels  33.3 us (90%)
  between operations  3.08 us (8%)
    pallas_call x1, Pallas kernels, local_step(): pl.pallas_call(functools.partial(exchange_kernel, sizes, peers, slots), o...  17.2 us
    pallas_call x1, Pallas kernels, local_step(): pl.pallas_call(functools.partial(total_kernel, sizes), out_shape=jax.Shap...  9.18 us
    pallas_call x1, Pallas kernels, local_step(): pl.pallas_call(functools.partial(force_kernel, sizes, peers, slots), out_...  7 us

profile of v5, /device:TPU:0, one launch (start us, length us, event | category | flops | bytes accessed | tf_op | source)
XLA Modules:
  0.0 36.5 jit_solution(4017414816345065871)
XLA Ops:
  1.3 17.2 %exchange.1 = (f32[16,768]{1,0:T(8,128)S(1)}, f32[17,4,768]{2,1,0:T(4,128)S(1)}, f32[17,4,256]{2,1,0:T(4,128)S(1)}) custom-call(f32[3,729]{1,0:T(4,128)} %bitcast.14, f32[3,729]{1,0:T(4,128)} %bitcast.15, f32[3,729]{1,0:T(4,128)} %bitcast.16, s32[729]{0:T(1024)} %id_hbm.1, s32[729]{0:T(1024)} %ok_hbm.1, f32[1,1]{1,0:T(1,128)} %bitcast.12.side_ref), custom_call_target="tpu_custom_call" | custom-call | tf_op jit(solution)/shard_map/exchange/pallas_call | solution.py:404
  18.6 7.0 %forces.1 = (f32[3,729]{1,0:T(4,128)}, f32[3,729]{1,0:T(4,128)}, f32[3,729]{1,0:T(4,128)}, s32[729]{0:T(1024)}, s32[729]{0:T(1024)}, /*index=5*/f32[1,128]{1,0:T(1,128)S(1)}) custom-call(f32[16,768]{1,0:T(8,128)S(1)} %get-tuple-element.15.srt_ref, f32[17,4,768]{2,1,0:T(4,128)S(1)} %get-tuple-element.16.gh_ref, f32[17,4,256]{2,1,0:T(4,128)S(1)} %get-tuple-element.17.ga_ref, ...), custom_call_target="tpu_custom_call" | custom-call | tf_op jit(solution)/shard_map/forces/pallas_call | solution.py:420
  25.6 9.2 %total.1 = f32[1,1]{1,0:T(1,128)} custom-call(f32[1,128]{1,0:T(1,128)S(1)} %get-tuple-element.23.part_ref), custom_call_target="tpu_custom_call" | custom-call | tf_op jit(solution)/shard_map/total/pallas_call | solution.py:429
  (4 shorter events, 0.1 us)

commit v6 on v5

--- a/solution.py
+++ b/solution.py
@@ -203,16 +203,16 @@
 
     staying = code == 13
     keys = bins_of(data)
-    for kind in range(2):
+    for kind in range(3):
         out3[kind] = sorted_block(data[0:8], keys[kind], staying)
     pl.semaphore_wait(barrier, len(peers))
     packets = []
     for index, d in enumerate(DIRS):
         row = pl.ds(index, 1)
         packets.append(send(pkt.at[row], rcv.at[row], psend.at[index], precv.at[index], (d[0] % size_x, d[1] % size_y, d[2] % size_z)))
-    blocks = send_blocks(out3, gh_ref, gsend, grecv, 0) + send_blocks(out3, gh_ref, gsend, grecv, 1)
-    out3[2] = sorted_block(data[0:8], keys[2], staying)
-    blocks = blocks + send_blocks(out3, gh_ref, gsend, grecv, 2)
+    blocks = []
+    for kind in range(3):
+        blocks = blocks + send_blocks(out3, gh_ref, gsend, grecv, kind)
     for copy in packets:
         copy.wait_recv()
 
@@ -221,9 +221,12 @@
     came_t = jnp.transpose(came)[0:16]
     came_ok = came_t[8:9] > 0.5
     keys = bins_of(came_t)
+    late = []
     for kind in range(3):
         new3[kind] = sorted_block(came_t[0:8], keys[kind], came_ok)
-        blocks = blocks + send_blocks(new3, ga_ref, asend, arecv, kind)
+        late = late + send_blocks(new3, ga_ref, asend, arecv, kind)
+    for copy in blocks:
+        copy.wait_recv()
 
     arr_ids = came[:, 6:7].astype(I32) * 65536 + came[:, 7:8].astype(I32)
     arr_ok = came[:, 8:9] > 0.5
@@ -237,7 +240,7 @@
     dest = jnp.where(jnp.concatenate([staying, came_ok], axis=1), rank.astype(I32), -1)
     srt_ref[...] = scatter_lanes(jnp.concatenate([data, came_t], axis=1), dest, slots)
 
-    for copy in blocks:
+    for copy in late:
         copy.wait_recv()
     for copy in sent:
         copy.wait_send()

time: 37.1 us -> 36.7 us (0.989); the launches traced: 36.5 us -> 36.8 us
    pallas_call x1, Pallas kernels: 9.18 us -> 10.4 us  [local_step(): pl.pallas_call(functools.partial(total_kernel, sizes), out_shape=jax.Shap...]
    pallas_call x1, Pallas kernels: 17.2 us -> 16.6 us  [local_step(): pl.pallas_call(functools.partial(exchange_kernel, sizes, peers, slots), o...]
where the time goes in v6:
time: 36.7 us; the launch traced here: 36.8 us
  Pallas kernels  33.6 us (92%)
  between operations  3.08 us (8%)
    pallas_call x1, Pallas kernels, local_step(): pl.pallas_call(functools.partial(exchange_kernel, sizes, peers, slots), o...  16.6 us
    pallas_call x1, Pallas kernels, local_step(): pl.pallas_call(functools.partial(total_kernel, sizes), out_shape=jax.Shap...  10.4 us
    pallas_call x1, Pallas kernels, local_step(): pl.pallas_call(functools.partial(force_kernel, sizes, peers, slots), out_...  6.67 us

profile of v6, /device:TPU:0, one launch (start us, length us, event | category | flops | bytes accessed | tf_op | source)
XLA Modules:
  0.0 36.8 jit_solution(1825702606475572018)
XLA Ops:
  1.3 16.6 %exchange.1 = (f32[16,768]{1,0:T(8,128)S(1)}, f32[17,4,768]{2,1,0:T(4,128)S(1)}, f32[17,4,256]{2,1,0:T(4,128)S(1)}) custom-call(f32[3,729]{1,0:T(4,128)} %bitcast.14, f32[3,729]{1,0:T(4,128)} %bitcast.15, f32[3,729]{1,0:T(4,128)} %bitcast.16, s32[729]{0:T(1024)} %id_hbm.1, s32[729]{0:T(1024)} %ok_hbm.1, f32[1,1]{1,0:T(1,128)} %bitcast.12.side_ref), custom_call_target="tpu_custom_call" | custom-call | tf_op jit(solution)/shard_map/exchange/pallas_call | solution.py:407
  18.0 6.7 %forces.1 = (f32[3,729]{1,0:T(4,128)}, f32[3,729]{1,0:T(4,128)}, f32[3,729]{1,0:T(4,128)}, s32[729]{0:T(1024)}, s32[729]{0:T(1024)}, /*index=5*/f32[1,128]{1,0:T(1,128)S(1)}) custom-call(f32[16,768]{1,0:T(8,128)S(1)} %get-tuple-element.15.srt_ref, f32[17,4,768]{2,1,0:T(4,128)S(1)} %get-tuple-element.16.gh_ref, f32[17,4,256]{2,1,0:T(4,128)S(1)} %get-tuple-element.17.ga_ref, ...), custom_call_target="tpu_custom_call" | custom-call | tf_op jit(solution)/shard_map/forces/pallas_call | solution.py:423
  24.6 10.4 %total.1 = f32[1,1]{1,0:T(1,128)} custom-call(f32[1,128]{1,0:T(1,128)S(1)} %get-tuple-element.23.part_ref), custom_call_target="tpu_custom_call" | custom-call | tf_op jit(solution)/shard_map/total/pallas_call | solution.py:432
  (4 shorter events, 0.1 us)

commit v7 on v6

--- a/solution.py
+++ b/solution.py
@@ -17,8 +17,8 @@
 NEAR = RC + 1.0e-3
 PACK = 8
 NEW = 256
-CHUNK = 4
-GROUPS = 4
+CHUNK = 3
+GROUPS = 8
 L = 128
 F32 = jnp.float32
 BF16 = jnp.bfloat16
@@ -111,7 +111,50 @@
     return jnp.concatenate([x, jnp.zeros((x.shape[0], width - x.shape[1]), x.dtype)], axis=1)
 
 
-def exchange_kernel(sizes, peers, slots, pos_hbm, vel_hbm, frc_hbm, id_hbm, ok_hbm, side_ref, srt_ref, gh_ref, ga_ref, pos_ref, vel_ref, frc_ref, id_ref, ok_ref, pkt, rcv, out3, new3, isem, psend, precv, gsend, grecv, asend, arecv):
+def pair_loop(own_cols, near_lanes, q, first, last, with_self, carry):
+    rows = [step_rows(q, g) for g in range(GROUPS)]
+    own = [[own_cols[rows[g], a * L:(a + 1) * L] for a in range(3)] for g in range(GROUPS)]
+
+    def body(c, carry):
+        force, en = [list(f) for f in carry[0]], carry[1]
+        for t in range(CHUNK):
+            place = pl.ds(pl.multiple_of((c * CHUNK + t) * L, L), L)
+            near_xyz = [near_lanes[a, :, place] for a in range(3)]
+            for g in range(GROUPS):
+                dx, dy, dz = [own[g][a] - near_xyz[a] for a in range(3)]
+                d2 = dx * dx + dy * dy + dz * dz
+                near = d2 < RC * RC
+                if with_self:
+                    near = near & (d2 > 0.0)
+                inv = jnp.where(near, lax.rsqrt(d2), 0.0)
+                s2 = inv * inv
+                s6 = s2 * s2 * s2
+                s12 = s6 * s6
+                p = s12 - s6
+                w = inv * (UPC / 24.0)
+                scale = (p + s12) * s2 + w
+                en = en + ((p + jnp.where(near, 0.25 * (RC * UPC - UCUT), 0.0)) - 6.0 * (w * d2))
+                force[g] = [force[g][0] + scale * dx, force[g][1] + scale * dy, force[g][2] + scale * dz]
+        return tuple(tuple(f) for f in force), en
+
+    return lax.fori_loop(first, last, body, carry)
+
+
+def step_rows(q, g):
+    return pl.ds(pl.multiple_of((q * GROUPS + g) * 8, 8), 8)
+
+
+def own_columns(xyz):
+    slots = xyz.shape[1]
+    parts = [part.astype(F32) for part in split3(xyz)]
+    parts = jnp.concatenate(parts + [jnp.zeros((7, slots), F32)], axis=0)
+    row = lax.broadcasted_iota(I32, (16, 3 * L), 0)
+    tile = lax.broadcasted_iota(I32, (16, 3 * L), 1) // L
+    picks = jnp.where((row == tile) | (row == tile + 3) | (row == tile + 6), 1.0, 0.0).astype(BF16)
+    return lax.dot_general(jnp.transpose(parts).astype(BF16), picks, NN, preferred_element_type=F32)
+
+
+def exchange_kernel(sizes, peers, slots, pos_hbm, vel_hbm, frc_hbm, id_hbm, ok_hbm, side_ref, srt_ref, gh_ref, ga_ref, own_ref, inner_ref, inner_en_ref, pos_ref, vel_ref, frc_ref, id_ref, ok_ref, pkt, rcv, out3, new3, lanes, isem, psend, precv, gsend, grecv, asend, arecv):
     size_x, size_y, size_z = sizes
     me = (lax.axis_index("x"), lax.axis_index("y"), lax.axis_index("z"))
 
@@ -238,7 +281,23 @@
     stay_place, _ = class_places(jnp.where(staying, 0, 31), False)
     rank = jnp.concatenate([stay_place, stay_below], axis=1) + arrivals_below
     dest = jnp.where(jnp.concatenate([staying, came_ok], axis=1), rank.astype(I32), -1)
-    srt_ref[...] = scatter_lanes(jnp.concatenate([data, came_t], axis=1), dest, slots)
+    merged = scatter_lanes(jnp.concatenate([data, came_t], axis=1), dest, slots)
+    srt_ref[...] = merged
+
+    good = merged[8:9] > 0.5
+    own_ref[...] = own_columns(jnp.where(good, merged[0:3], -FAR))
+    for a in range(3):
+        lanes[a] = jnp.broadcast_to(jnp.where(good, merged[a:a + 1], FAR), (8, slots))
+    zero = jnp.zeros((8, L), F32)
+
+    def own_step(q, energy):
+        force, energy = pair_loop(own_ref, lanes, q, 0, slots // (CHUNK * L), True, (((zero,) * 3,) * GROUPS, energy))
+        for g in range(GROUPS):
+            for a in range(3):
+                inner_ref[a, step_rows(q, g), :] = force[g][a]
+        return energy
+
+    inner_en_ref[...] = lax.fori_loop(0, slots // (8 * GROUPS), own_step, zero)
 
     for copy in late:
         copy.wait_recv()
@@ -246,7 +305,7 @@
         copy.wait_send()
 
 
-def force_kernel(sizes, peers, slots, srt_ref, gh_ref, ga_ref, offs_ref, side_ref, pos_ref, vel_ref, frc_ref, id_ref, ok_ref, en_ref, line, wide_line, own_cols, sums):
+def force_kernel(sizes, peers, slots, srt_ref, gh_ref, ga_ref, own_cols, inner_ref, inner_en_ref, offs_ref, side_ref, pos_ref, vel_ref, frc_ref, id_ref, ok_ref, en_ref, line, wide_line, sums):
     size_x, size_y, size_z = sizes
     me = (lax.axis_index("x"), lax.axis_index("y"), lax.axis_index("z"))
     n = pos_ref.shape[1]
@@ -257,18 +316,10 @@
     spread = side > 2.0 * NEAR
     span = slots + L
 
-    parts = [part.astype(F32) for part in split3(jnp.where(good, srt_ref[0:3], -FAR))]
-    parts = jnp.concatenate(parts + [jnp.zeros((7, slots), F32)], axis=0)
-    row = lax.broadcasted_iota(I32, (16, 3 * L), 0)
-    tile = lax.broadcasted_iota(I32, (16, 3 * L), 1) // L
-    picks = jnp.where((row == tile) | (row == tile + 3) | (row == tile + 6), 1.0, 0.0).astype(BF16)
-    own_cols[...] = lax.dot_general(jnp.transpose(parts).astype(BF16), picks, NN, preferred_element_type=F32)
-
-    pad5 = jnp.zeros((5, slots), F32)
     away = jnp.full((8, L), FAR, F32)
-    line[:, 0:span] = jnp.concatenate([jnp.concatenate([jnp.where(good, srt_ref[0:3], FAR), pad5], axis=0), away], axis=1)
+    line[:, 0:L] = away
     lane = lax.broadcasted_iota(I32, (8, span), 1)
-    fill = count
+    fill = jnp.int32(0)
     for d in DIRS:
         offset = (d[0] % size_x, d[1] % size_y, d[2] % size_z)
         back = ((-offset[0]) % size_x, (-offset[1]) % size_y, (-offset[2]) % size_z)
@@ -299,7 +350,6 @@
             fill = fill + (end - begin)
     rest = pl.multiple_of(((fill + L - 1) // L) * L, L)
     line[:, pl.ds(rest, CHUNK * L)] = jnp.full((8, CHUNK * L), FAR, F32)
-    self_chunks = (count + CHUNK * L - 1) // (CHUNK * L)
     chunks = (fill + CHUNK * L - 1) // (CHUNK * L)
 
     def widen(c, carry):
@@ -313,42 +363,15 @@
     lax.fori_loop(0, chunks, widen, 0)
 
     def own_step(q, energy):
-        rows = [pl.ds(pl.multiple_of((q * GROUPS + g) * 8, 8), 8) for g in range(GROUPS)]
-        own = [[own_cols[rows[g], a * L:a * L + L] for a in range(3)] for g in range(GROUPS)]
-
-        def body(with_self, c, carry):
-            force, en = [list(f) for f in carry[0]], carry[1]
-            for t in range(CHUNK):
-                place = pl.ds(pl.multiple_of((c * CHUNK + t) * L, L), L)
-                near_xyz = [wide_line[a, :, place] for a in range(3)]
-                for g in range(GROUPS):
-                    dx, dy, dz = [own[g][a] - near_xyz[a] for a in range(3)]
-                    d2 = dx * dx + dy * dy + dz * dz
-                    near = d2 < RC * RC
-                    if with_self:
-                        near = near & (d2 > 0.0)
-                    inv = jnp.where(near, lax.rsqrt(d2), 0.0)
-                    s2 = inv * inv
-                    s6 = s2 * s2 * s2
-                    s12 = s6 * s6
-                    p = s12 - s6
-                    w = inv * (UPC / 24.0)
-                    scale = (p + s12) * s2 + w
-                    en = en + ((p + jnp.where(near, 0.25 * (RC * UPC - UCUT), 0.0)) - 6.0 * (w * d2))
-                    force[g] = [force[g][0] + scale * dx, force[g][1] + scale * dy, force[g][2] + scale * dz]
-            return tuple(tuple(f) for f in force), en
-
-        zero = jnp.zeros((8, L), F32)
-        carry = (((zero,) * 3,) * GROUPS, energy)
-        carry = lax.fori_loop(0, self_chunks, functools.partial(body, True), carry)
-        force, energy = lax.fori_loop(self_chunks, chunks, functools.partial(body, False), carry)
+        start = tuple(tuple(inner_ref[a, step_rows(q, g), :] for a in range(3)) for g in range(GROUPS))
+        force, energy = pair_loop(own_cols, wide_line, q, 0, chunks, False, (start, energy))
         for g in range(GROUPS):
             for a in range(3):
-                sums[a, rows[g], :] = force[g][a]
+                sums[a, step_rows(q, g), :] = force[g][a]
         return energy
 
     own_steps = (count + 8 * GROUPS - 1) // (8 * GROUPS)
-    energy = lax.fori_loop(0, own_steps, own_step, jnp.zeros((8, L), F32))
+    energy = lax.fori_loop(0, own_steps, own_step, inner_en_ref[...])
     en_ref[...] = 2.0 * jnp.sum(energy, axis=0, keepdims=True)
 
     col = lax.broadcasted_iota(I32, (L, L), 1)
@@ -404,14 +427,15 @@
         side = jnp.reshape(brick_side, (1, 1))
         vmem = pl.BlockSpec(memory_space=pltpu.VMEM)
         smem = pl.BlockSpec(memory_space=pltpu.SMEM)
-        srt, ghosts, fresh = pl.pallas_call(
+        srt, ghosts, fresh, own, inner, inner_en = pl.pallas_call(
             functools.partial(exchange_kernel, sizes, peers, slots),
-            out_shape=(jax.ShapeDtypeStruct((16, slots), F32), jax.ShapeDtypeStruct((len(peers), 4, slots), F32), jax.ShapeDtypeStruct((len(peers), 4, NEW), F32)),
+            out_shape=(jax.ShapeDtypeStruct((16, slots), F32), jax.ShapeDtypeStruct((len(peers), 4, slots), F32), jax.ShapeDtypeStruct((len(peers), 4, NEW), F32),
+                       jax.ShapeDtypeStruct((slots, 3 * L), F32), jax.ShapeDtypeStruct((3, slots, L), F32), jax.ShapeDtypeStruct((8, L), F32)),
             in_specs=[pl.BlockSpec(memory_space=pltpu.HBM)] * 5 + [smem],
-            out_specs=(vmem,) * 3,
+            out_specs=(vmem,) * 6,
             scratch_shapes=[
                 pltpu.VMEM((3, n), F32), pltpu.VMEM((3, n), F32), pltpu.VMEM((3, n), F32), pltpu.VMEM((n,), I32), pltpu.VMEM((n,), I32),
-                pltpu.VMEM((32, L), F32), pltpu.VMEM((26, L), F32), pltpu.VMEM((3, 4, slots), F32), pltpu.VMEM((3, 4, NEW), F32),
+                pltpu.VMEM((32, L), F32), pltpu.VMEM((26, L), F32), pltpu.VMEM((3, 4, slots), F32), pltpu.VMEM((3, 4, NEW), F32), pltpu.VMEM((3, 8, slots), F32),
                 pltpu.SemaphoreType.DMA((5,)), pltpu.SemaphoreType.DMA((26,)), pltpu.SemaphoreType.DMA((26,)),
             ] + [pltpu.SemaphoreType.DMA((len(peers),))] * 4,
             compiler_params=pltpu.CompilerParams(collective_id=0, has_side_effects=True, vmem_limit_bytes=40 * 2 ** 20),
@@ -423,12 +447,12 @@
         new_pos, new_vel, new_frc, new_id, new_ok, energy = pl.pallas_call(
             functools.partial(force_kernel, sizes, peers, slots),
             out_shape=(out_f, out_f, out_f, out_i, out_i, jax.ShapeDtypeStruct((1, L), F32)),
-            in_specs=[vmem] * 3 + [smem] * 2,
+            in_specs=[vmem] * 6 + [smem] * 2,
             out_specs=(vmem,) * 6,
-            scratch_shapes=[pltpu.VMEM((8, 28 * slots + CHUNK * L), F32), pltpu.VMEM((3, 8, 28 * slots + CHUNK * L), F32), pltpu.VMEM((slots, 3 * L), F32), pltpu.VMEM((3, slots, L), F32)],
+            scratch_shapes=[pltpu.VMEM((8, 28 * slots + CHUNK * L), F32), pltpu.VMEM((3, 8, 28 * slots + CHUNK * L), F32), pltpu.VMEM((3, slots, L), F32)],
             compiler_params=pltpu.CompilerParams(vmem_limit_bytes=40 * 2 ** 20),
             name="forces",
-        )(srt, ghosts, fresh, offs, side)
+        )(srt, ghosts, fresh, own, inner, inner_en, offs, side)
         energy = pl.pallas_call(
             functools.partial(total_kernel, sizes),
             out_shape=jax.ShapeDtypeStruct((1, 1), F32),

time: 36.7 us -> 37 us (level)
    pallas_call x1, Pallas kernels: 16.6 us -> 17.6 us  [local_step(): pl.pallas_call(functools.partial(exchange_kernel, sizes, peers, slots), o...]
    pallas_call x1, Pallas kernels: 6.67 us -> 5.7 us  [local_step(): pl.pallas_call(functools.partial(force_kernel, sizes, peers, slots), out_...]
where the time goes in v7:
time: 37 us; the launch traced here: 36.7 us
  Pallas kernels  33.6 us (91%)
  between operations  3.08 us (8%)
    pallas_call x1, Pallas kernels, local_step(): pl.pallas_call(functools.partial(exchange_kernel, sizes, peers, slots), o...  17.6 us
    pallas_call x1, Pallas kernels, local_step(): pl.pallas_call(functools.partial(total_kernel, sizes), out_shape=jax.Shap...  10.3 us
    pallas_call x1, Pallas kernels, local_step(): pl.pallas_call(functools.partial(force_kernel, sizes, peers, slots), out_...  5.7 us

profile of v7, /device:TPU:0, one launch (start us, length us, event | category | flops | bytes accessed | tf_op | source)
XLA Modules:
  0.0 36.7 jit_solution(592715985789915124)
XLA Ops:
  1.3 17.6 %exchange.1 = (f32[16,768]{1,0:T(8,128)S(1)}, f32[17,4,768]{2,1,0:T(4,128)S(1)}, f32[17,4,256]{2,1,0:T(4,128)S(1)}, f32[768,384]{1,0:T(8,128)S(1)}, f32[3,768,128]{2,1,0:T(8,128)S(1)}, /*index=5*/f32[8,128]{1,0:T(8,128)S(1)}) custom-call(f32[3,729]{1,0:T(4,128)} %bitcast.14, f32[3,729]{1,0:T(4,128)} %bitcast.15, f32[3,729]{1,0:T(4,128)} %bitcast.16, ...), custom_call_target="tpu_custom_call" | custom-call | tf_op jit(solution)/shard_map/exchange/pallas_call | solution.py:430
  19.0 5.7 %forces.1 = (f32[3,729]{1,0:T(4,128)}, f32[3,729]{1,0:T(4,128)}, f32[3,729]{1,0:T(4,128)}, s32[729]{0:T(1024)}, s32[729]{0:T(1024)}, /*index=5*/f32[1,128]{1,0:T(1,128)S(1)}) custom-call(f32[16,768]{1,0:T(8,128)S(1)} %get-tuple-element.18.srt_ref, f32[17,4,768]{2,1,0:T(4,128)S(1)} %get-tuple-element.19.gh_ref, f32[17,4,256]{2,1,0:T(4,128)S(1)} %get-tuple-element.20.ga_ref, ...), custom_call_target="tpu_custom_call" | custom-call | tf_op jit(solution)/shard_map/forces/pallas_call | solution.py:447
  24.7 10.3 %total.1 = f32[1,1]{1,0:T(1,128)} custom-call(f32[1,128]{1,0:T(1,128)S(1)} %get-tuple-element.29.part_ref), custom_call_target="tpu_custom_call" | custom-call | tf_op jit(solution)/shard_map/total/pallas_call | solution.py:456
  (4 shorter events, 0.1 us)

commit v8 on v7

--- a/solution.py
+++ b/solution.py
@@ -15,11 +15,13 @@
 MESH_AXES = ("z", "y", "x")
 DIRS = [(dx, dy, dz) for dz in (-1, 0, 1) for dy in (-1, 0, 1) for dx in (-1, 0, 1) if (dx, dy, dz) != (0, 0, 0)]
 NEAR = RC + 1.0e-3
+MAJOR = ((2, 1, 0), (1, 0, 2), (0, 2, 1))
 PACK = 8
 NEW = 256
 CHUNK = 3
 GROUPS = 8
 L = 128
+TILE = (8, L)
 F32 = jnp.float32
 BF16 = jnp.bfloat16
 I32 = jnp.int32
@@ -34,21 +36,13 @@
 
 
 def range_of(d):
-    cx, cy, cz = [(1, 0, 2)[c] for c in (d[0], d[1], d[2])]
-    kind = order_of(d)
-    if kind == 0:
-        if d[0] == 0 and d[1] == 0:
-            return cz * 9, cz * 9 + 9
-        if d[0] == 0:
-            return cz * 9 + cy * 3, cz * 9 + cy * 3 + 3
-        return cz * 9 + cy * 3 + cx, cz * 9 + cy * 3 + cx + 1
-    if kind == 1:
-        if d[0] == 0:
-            return cy * 9, cy * 9 + 9
-        return cy * 9 + cx * 3, cy * 9 + cx * 3 + 3
-    if d[2] == 0:
-        return cx * 9, cx * 9 + 9
-    return cx * 9 + cz * 3, cx * 9 + cz * 3 + 3
+    first, size = 0, 27
+    for axis in MAJOR[order_of(d)]:
+        if d[axis] == 0:
+            break
+        size = size // 3
+        first = first + (1, 0, 2)[d[axis]] * size
+    return first, first + size
 
 
 def split3(x):
@@ -213,8 +207,7 @@
         for axis in range(3):
             loc = pos[axis:axis + 1] - low_side[axis]
             bins.append(jnp.where(loc < NEAR, 0, jnp.where(loc > side - NEAR, 2, 1)))
-        cx, cy, cz = bins
-        return cz * 9 + cy * 3 + cx, cy * 9 + cx * 3 + cz, cx * 9 + cz * 3 + cy
+        return [(bins[i] * 3 + bins[j]) * 3 + bins[k] for i, j, k in MAJOR]
 
     eye = lax.broadcasted_iota(I32, (32, L), 0) == lax.broadcasted_iota(I32, (32, L), 1)
 
@@ -286,12 +279,13 @@
 
     good = merged[8:9] > 0.5
     own_ref[...] = own_columns(jnp.where(good, merged[0:3], -FAR))
+    first = CHUNK * L
     for a in range(3):
-        lanes[a] = jnp.broadcast_to(jnp.where(good, merged[a:a + 1], FAR), (8, slots))
-    zero = jnp.zeros((8, L), F32)
+        lanes[a] = jnp.broadcast_to(jnp.where(good, merged[a:a + 1], FAR)[:, 0:first], (8, first))
+    zero = jnp.zeros(TILE, F32)
 
     def own_step(q, energy):
-        force, energy = pair_loop(own_ref, lanes, q, 0, slots // (CHUNK * L), True, (((zero,) * 3,) * GROUPS, energy))
+        force, energy = pair_loop(own_ref, lanes, q, 0, 1, True, (((zero,) * 3,) * GROUPS, energy))
         for g in range(GROUPS):
             for a in range(3):
                 inner_ref[a, step_rows(q, g), :] = force[g][a]
@@ -316,15 +310,16 @@
     spread = side > 2.0 * NEAR
     span = slots + L
 
-    away = jnp.full((8, L), FAR, F32)
-    line[:, 0:L] = away
+    away = jnp.full(TILE, FAR, F32)
+    first = CHUNK * L
+    line[:, 0:slots - first] = jnp.concatenate([jnp.where(good, srt_ref[0:3], FAR), jnp.full((5, slots), FAR, F32)], axis=0)[:, first:]
     lane = lax.broadcasted_iota(I32, (8, span), 1)
-    fill = jnp.int32(0)
+    fill = jnp.maximum(count - first, 0)
     for d in DIRS:
         offset = (d[0] % size_x, d[1] % size_y, d[2] % size_z)
         back = ((-offset[0]) % size_x, (-offset[1]) % size_y, (-offset[2]) % size_z)
         index = peers.index(back)
-        first, last = range_of(d)
+        low, high = range_of(d)
         shifts = []
         for axis in range(3):
             box = side * float(sizes[axis])
@@ -336,8 +331,8 @@
                 shifts.append(jnp.float32(0.0))
         for source, entry in ((gh_ref, index), (ga_ref, index + len(peers))):
             width = source.shape[2]
-            begin = jnp.where(spread, offs_ref[entry, first], 0)
-            end = jnp.where(spread, offs_ref[entry, last], offs_ref[entry, 27])
+            begin = jnp.where(spread, offs_ref[entry, low], 0)
+            end = jnp.where(spread, offs_ref[entry, high], offs_ref[entry, 27])
             block = jnp.concatenate([source[index, a:a + 1] + shifts[a] for a in range(3)] + [jnp.zeros((5, width), F32)], axis=0)
             block = jnp.concatenate([block, away], axis=1)
             head = fill & (L - 1)
@@ -350,21 +345,22 @@
             fill = fill + (end - begin)
     rest = pl.multiple_of(((fill + L - 1) // L) * L, L)
     line[:, pl.ds(rest, CHUNK * L)] = jnp.full((8, CHUNK * L), FAR, F32)
-    chunks = (fill + CHUNK * L - 1) // (CHUNK * L)
+    chunks = jnp.maximum((fill + CHUNK * L - 1) // (CHUNK * L), 1)
 
     def widen(c, carry):
         for t in range(CHUNK):
             place = pl.ds(pl.multiple_of((c * CHUNK + t) * L, L), L)
             tile = line[:, place]
             for a in range(3):
-                wide_line[a, :, place] = jnp.broadcast_to(tile[a:a + 1], (8, L))
+                wide_line[a, :, place] = jnp.broadcast_to(tile[a:a + 1], TILE)
         return carry
 
     lax.fori_loop(0, chunks, widen, 0)
 
     def own_step(q, energy):
         start = tuple(tuple(inner_ref[a, step_rows(q, g), :] for a in range(3)) for g in range(GROUPS))
-        force, energy = pair_loop(own_cols, wide_line, q, 0, chunks, False, (start, energy))
+        carry = pair_loop(own_cols, wide_line, q, 0, 1, True, (start, energy))
+        force, energy = pair_loop(own_cols, wide_line, q, 1, chunks, False, carry)
         for g in range(GROUPS):
             for a in range(3):
                 sums[a, step_rows(q, g), :] = force[g][a]
@@ -430,12 +426,12 @@
         srt, ghosts, fresh, own, inner, inner_en = pl.pallas_call(
             functools.partial(exchange_kernel, sizes, peers, slots),
             out_shape=(jax.ShapeDtypeStruct((16, slots), F32), jax.ShapeDtypeStruct((len(peers), 4, slots), F32), jax.ShapeDtypeStruct((len(peers), 4, NEW), F32),
-                       jax.ShapeDtypeStruct((slots, 3 * L), F32), jax.ShapeDtypeStruct((3, slots, L), F32), jax.ShapeDtypeStruct((8, L), F32)),
+                       jax.ShapeDtypeStruct((slots, 3 * L), F32), jax.ShapeDtypeStruct((3, slots, L), F32), jax.ShapeDtypeStruct(TILE, F32)),
             in_specs=[pl.BlockSpec(memory_space=pltpu.HBM)] * 5 + [smem],
             out_specs=(vmem,) * 6,
             scratch_shapes=[
                 pltpu.VMEM((3, n), F32), pltpu.VMEM((3, n), F32), pltpu.VMEM((3, n), F32), pltpu.VMEM((n,), I32), pltpu.VMEM((n,), I32),
-                pltpu.VMEM((32, L), F32), pltpu.VMEM((26, L), F32), pltpu.VMEM((3, 4, slots), F32), pltpu.VMEM((3, 4, NEW), F32), pltpu.VMEM((3, 8, slots), F32),
+                pltpu.VMEM((32, L), F32), pltpu.VMEM((26, L), F32), pltpu.VMEM((3, 4, slots), F32), pltpu.VMEM((3, 4, NEW), F32), pltpu.VMEM((3, 8, CHUNK * L), F32),
                 pltpu.SemaphoreType.DMA((5,)), pltpu.SemaphoreType.DMA((26,)), pltpu.SemaphoreType.DMA((26,)),
             ] + [pltpu.SemaphoreType.DMA((len(peers),))] * 4,
             compiler_params=pltpu.CompilerParams(collective_id=0, has_side_effects=True, vmem_limit_bytes=40 * 2 ** 20),

time: 37 us -> 35.4 us (0.957)
  Pallas kernels: 33.6 us -> 32.1 us
    pallas_call x1, Pallas kernels: 10.3 us -> 8.88 us  [local_step(): pl.pallas_call(functools.partial(total_kernel, sizes), out_shape=jax.Shap...]
    pallas_call x1, Pallas kernels: 17.6 us -> 16.6 us  [local_step(): pl.pallas_call(functools.partial(exchange_kernel, sizes, peers, slots), o...]
    pallas_call x1, Pallas kernels: 5.7 us -> 6.66 us  [local_step(): pl.pallas_call(functools.partial(force_kernel, sizes, peers, slots), out_...]
where the time goes in v8:
time: 35.4 us; the launch traced here: 35.3 us
  Pallas kernels  32.1 us (91%)
  between operations  3.08 us (9%)
    pallas_call x1, Pallas kernels, local_step(): pl.pallas_call(functools.partial(exchange_kernel, sizes, peers, slots), o...  16.6 us
    pallas_call x1, Pallas kernels, local_step(): pl.pallas_call(functools.partial(total_kernel, sizes), out_shape=jax.Shap...  8.88 us
    pallas_call x1, Pallas kernels, local_step(): pl.pallas_call(functools.partial(force_kernel, sizes, peers, slots), out_...  6.66 us

profile of v8, /device:TPU:0, one launch (start us, length us, event | category | flops | bytes accessed | tf_op | source)
XLA Modules:
  0.0 35.3 jit_solution(18047676875721227902)
XLA Ops:
  1.3 16.6 %exchange.1 = (f32[16,768]{1,0:T(8,128)S(1)}, f32[17,4,768]{2,1,0:T(4,128)S(1)}, f32[17,4,256]{2,1,0:T(4,128)S(1)}, f32[768,384]{1,0:T(8,128)S(1)}, f32[3,768,128]{2,1,0:T(8,128)S(1)}, /*index=5*/f32[8,128]{1,0:T(8,128)S(1)}) custom-call(f32[3,729]{1,0:T(4,128)} %bitcast.14, f32[3,729]{1,0:T(4,128)} %bitcast.15, f32[3,729]{1,0:T(4,128)} %bitcast.16, ...), custom_call_target="tpu_custom_call" | custom-call | tf_op jit(solution)/shard_map/exchange/pallas_call | solution.py:426
  18.0 6.7 %forces.1 = (f32[3,729]{1,0:T(4,128)}, f32[3,729]{1,0:T(4,128)}, f32[3,729]{1,0:T(4,128)}, s32[729]{0:T(1024)}, s32[729]{0:T(1024)}, /*index=5*/f32[1,128]{1,0:T(1,128)S(1)}) custom-call(f32[16,768]{1,0:T(8,128)S(1)} %get-tuple-element.18.srt_ref, f32[17,4,768]{2,1,0:T(4,128)S(1)} %get-tuple-element.19.gh_ref, f32[17,4,256]{2,1,0:T(4,128)S(1)} %get-tuple-element.20.ga_ref, ...), custom_call_target="tpu_custom_call" | custom-call | tf_op jit(solution)/shard_map/forces/pallas_call | solution.py:443
  24.6 8.9 %total.1 = f32[1,1]{1,0:T(1,128)} custom-call(f32[1,128]{1,0:T(1,128)S(1)} %get-tuple-element.29.part_ref), custom_call_target="tpu_custom_call" | custom-call | tf_op jit(solution)/shard_map/total/pallas_call | solution.py:452
  (4 shorter events, 0.1 us)

commit v9 on v8

--- a/solution.py
+++ b/solution.py
@@ -220,14 +220,11 @@
         counts = jnp.sum(jnp.where(eye, before, 0.0), axis=0, keepdims=True)
         return jnp.concatenate([jnp.where(lane < total, arranged[0:3], FAR), pad_lanes(counts, width)], axis=0)
 
-    sent = []
-
     def send(src, dst, ssem, rsem, offset):
         copy = pltpu.make_async_remote_copy(
             src_ref=src, dst_ref=dst, send_sem=ssem, recv_sem=rsem,
             device_id=device_at(offset), device_id_type=pl.DeviceIdType.MESH)
         copy.start()
-        sent.append(copy)
         return copy
 
     def send_blocks(block, dst, ssem, rsem, kind):
@@ -261,8 +258,8 @@
     for kind in range(3):
         new3[kind] = sorted_block(came_t[0:8], keys[kind], came_ok)
         late = late + send_blocks(new3, ga_ref, asend, arecv, kind)
-    for copy in blocks:
-        copy.wait_recv()
+    for copy in packets:
+        copy.wait_send()
 
     arr_ids = came[:, 6:7].astype(I32) * 65536 + came[:, 7:8].astype(I32)
     arr_ok = came[:, 8:9] > 0.5
@@ -293,10 +290,8 @@
 
     inner_en_ref[...] = lax.fori_loop(0, slots // (8 * GROUPS), own_step, zero)
 
-    for copy in late:
-        copy.wait_recv()
-    for copy in sent:
-        copy.wait_send()
+    for copy in blocks + late:
+        copy.wait()
 
 
 def force_kernel(sizes, peers, slots, srt_ref, gh_ref, ga_ref, own_cols, inner_ref, inner_en_ref, offs_ref, side_ref, pos_ref, vel_ref, frc_ref, id_ref, ok_ref, en_ref, line, wide_line, sums):
@@ -389,6 +384,7 @@
     me = (lax.axis_index("x"), lax.axis_index("y"), lax.axis_index("z"))
     mine = (me[2] * size_y + me[1]) * size_x + me[0]
     others = [(dx, dy, dz) for dz in range(size_z) for dy in range(size_y) for dx in range(size_x) if dx + dy + dz > 0]
+    others.sort(key=lambda o: -(2 * min(o[2], size_z - o[2]) + 2 * o[1] + min(o[0], size_x - o[0])))
 
     def device_at(offset):
         return (lax.rem(me[2] + offset[2], size_z), lax.rem(me[1] + offset[1], size_y), lax.rem(me[0] + offset[0], size_x))

time: 35.4 us -> 35.1 us (level)
  Pallas kernels: 32.1 us -> 31.7 us
    pallas_call x1, Pallas kernels: 8.88 us -> 8.52 us  [local_step(): pl.pallas_call(functools.partial(total_kernel, sizes), out_shape=jax.Shap...]
where the time goes in v9:
time: 35.1 us; the launch traced here: 34.8 us
  Pallas kernels  31.7 us (90%)
  between operations  3.08 us (9%)
    pallas_call x1, Pallas kernels, local_step(): pl.pallas_call(functools.partial(exchange_kernel, sizes, peers, slots), o...  16.5 us
    pallas_call x1, Pallas kernels, local_step(): pl.pallas_call(functools.partial(total_kernel, sizes), out_shape=jax.Shap...  8.52 us
    pallas_call x1, Pallas kernels, local_step(): pl.pallas_call(functools.partial(force_kernel, sizes, peers, slots), out_...  6.65 us

profile of v9, /device:TPU:0, one launch (start us, length us, event | category | flops | bytes accessed | tf_op | source)
XLA Modules:
  0.0 34.8 jit_solution(7037358515180092193)
XLA Ops:
  1.3 16.5 %exchange.1 = (f32[16,768]{1,0:T(8,128)S(1)}, f32[17,4,768]{2,1,0:T(4,128)S(1)}, f32[17,4,256]{2,1,0:T(4,128)S(1)}, f32[768,384]{1,0:T(8,128)S(1)}, f32[3,768,128]{2,1,0:T(8,128)S(1)}, /*index=5*/f32[8,128]{1,0:T(8,128)S(1)}) custom-call(f32[3,729]{1,0:T(4,128)} %bitcast.14, f32[3,729]{1,0:T(4,128)} %bitcast.15, f32[3,729]{1,0:T(4,128)} %bitcast.16, ...), custom_call_target="tpu_custom_call" | custom-call | tf_op jit(solution)/shard_map/exchange/pallas_call | solution.py:422
  17.9 6.7 %forces.1 = (f32[3,729]{1,0:T(4,128)}, f32[3,729]{1,0:T(4,128)}, f32[3,729]{1,0:T(4,128)}, s32[729]{0:T(1024)}, s32[729]{0:T(1024)}, /*index=5*/f32[1,128]{1,0:T(1,128)S(1)}) custom-call(f32[16,768]{1,0:T(8,128)S(1)} %get-tuple-element.18.srt_ref, f32[17,4,768]{2,1,0:T(4,128)S(1)} %get-tuple-element.19.gh_ref, f32[17,4,256]{2,1,0:T(4,128)S(1)} %get-tuple-element.20.ga_ref, ...), custom_call_target="tpu_custom_call" | custom-call | tf_op jit(solution)/shard_map/forces/pallas_call | solution.py:439
  24.5 8.5 %total.1 = f32[1,1]{1,0:T(1,128)} custom-call(f32[1,128]{1,0:T(1,128)S(1)} %get-tuple-element.29.part_ref), custom_call_target="tpu_custom_call" | custom-call | tf_op jit(solution)/shard_map/total/pallas_call | solution.py:448
  (4 shorter events, 0.1 us)
